TPU v7x, 16 devices: a 4x2x1 block of a 4x4x8 slice. The times are simulated.
16 devices in a mesh: data: 2 (over y, z), model: 8 (over x, core).
Axes of the slice: x: 4, y: 2, z: 1, core: 2. Of those that a mesh axis runs over, the one named last changes fastest.
The devices are a block of a 4x4x8 slice.
Arguments:
- tokens: bfloat16 [16, 192, 3072], P('data'), parts along dimension 0
- seg_ids: int32 [16, 192], P('data'), parts along dimension 0
- d_out: bfloat16 [16, 192, 3072], P('data'), parts along dimension 0
- gain_attn: bfloat16 [3072], replicated
- gain_mlp: bfloat16 [3072], replicated
- w_qkv: bfloat16 [3072, 24, 3, 128], P(None, 'model')
- w_out: bfloat16 [24, 128, 3072], P('model')
- w_up: bfloat16 [3072, 8192], P(None, 'model')
- w_down: bfloat16 [8192, 3072], P('model')
Outputs:
- output 1: bfloat16 [16, 192, 3072], P('data'), parts along dimension 0
- output 2: bfloat16 [16, 192, 3072], P('data'), parts along dimension 0
- output 3: bfloat16 [6144, 24, 3, 128], P('data', 'model'), parts along dimension 0
- output 4: bfloat16 [48, 128, 3072], P(('data', 'model')), parts along dimension 0
- output 5: bfloat16 [6144, 8192], P('data', 'model'), parts along dimension 0
- output 6: bfloat16 [16384, 3072], P(('data', 'model')), parts along dimension 0
- output 7: float32 [6144], P('data'), parts along dimension 0
- output 8: float32 [6144], P('data'), parts along dimension 0
There are 2 independent parts. A program takes and returns all parts, laid end to end along the dimension named above; an argument that names none is the same for every part.
All inputs are finite; a program needn't handle non-finite values.
Results may differ from a plain program's by a relative error of at most 0.02.
Values are sent between devices in bfloat16 or wider.
A program may use at most 768 MiB of HBM per device.

v0:
```python
import functools
import jax
import jax.numpy as jnp
from jax import lax
from jax.sharding import PartitionSpec as P

NORM_EPS = 1e-5


def layer_norm(values, gain_vec):
    mean_val = jnp.mean(values, axis=-1, keepdims=True)
    centered = values - mean_val
    var_val = jnp.mean(centered * centered, axis=-1, keepdims=True)
    return centered * lax.rsqrt(var_val + NORM_EPS) * gain_vec


def causal_mask(seg_ids):
    seq_len = seg_ids.shape[-1]
    query_pos = lax.broadcasted_iota(jnp.int32, (seq_len, seq_len), 0)
    key_pos = lax.broadcasted_iota(jnp.int32, (seq_len, seq_len), 1)
    same_doc = seg_ids[:, :, None] == seg_ids[:, None, :]
    return (same_doc & (query_pos >= key_pos)[None])[:, None]


def forward_pass(tokens, allowed, gain_attn, gain_mlp, w_qkv, w_out, w_up, w_down, reduce_sum):
    head_dim = w_qkv.shape[3]
    x_f32 = tokens.astype(jnp.float32)
    normed = layer_norm(x_f32, gain_attn.astype(jnp.float32)).astype(jnp.bfloat16)
    qkv_all = jnp.einsum('bsh,hnjd->jbnsd', normed, w_qkv, preferred_element_type=jnp.float32).astype(jnp.bfloat16)
    scores = jnp.einsum('bnqd,bnkd->bnqk', qkv_all[0], qkv_all[1], preferred_element_type=jnp.float32) * (head_dim ** -0.5)
    attn_probs = jax.nn.softmax(jnp.where(allowed, scores, -1e30), axis=-1)
    probs_bf = attn_probs.astype(jnp.bfloat16)
    attn_heads = jnp.einsum('bnqk,bnkd->bnqd', probs_bf, qkv_all[2], preferred_element_type=jnp.float32).astype(jnp.bfloat16)
    attn_proj = reduce_sum(jnp.einsum('bnsd,ndh->bsh', attn_heads, w_out, preferred_element_type=jnp.float32).astype(jnp.bfloat16))
    resid_f32 = (x_f32 + attn_proj.astype(jnp.float32)).astype(jnp.bfloat16).astype(jnp.float32)
    normed_mlp = layer_norm(resid_f32, gain_mlp.astype(jnp.float32)).astype(jnp.bfloat16)
    pre_act = jnp.einsum('bsh,hf->bsf', normed_mlp, w_up, preferred_element_type=jnp.float32)
    hidden = jax.nn.gelu(pre_act, approximate=True).astype(jnp.bfloat16)
    mlp_down = reduce_sum(jnp.einsum('bsf,fh->bsh', hidden, w_down, preferred_element_type=jnp.float32).astype(jnp.bfloat16))
    layer_out = (resid_f32 + mlp_down.astype(jnp.float32)).astype(jnp.bfloat16)
    saved = dict(normed=normed, qkv_all=qkv_all, attn_probs=attn_probs, probs_bf=probs_bf, attn_heads=attn_heads, resid_f32=resid_f32, normed_mlp=normed_mlp, pre_act=pre_act, hidden=hidden)
    return layer_out, saved


def backward_pass(tokens, d_out, gain_attn, gain_mlp, w_qkv, w_out, w_up, w_down, saved, reduce_sum):
    head_dim = w_qkv.shape[3]
    qkv_all = saved['qkv_all']
    attn_probs = saved['attn_probs']
    d_hidden = jnp.einsum('bsh,fh->bsf', d_out, w_down, preferred_element_type=jnp.float32).astype(jnp.bfloat16)
    d_w_down = jnp.einsum('bsf,bsh->fh', saved['hidden'], d_out, preferred_element_type=jnp.float32).astype(jnp.bfloat16)
    _, gelu_back = jax.vjp(functools.partial(jax.nn.gelu, approximate=True), saved['pre_act'])
    d_pre = gelu_back(d_hidden.astype(jnp.float32))[0].astype(jnp.bfloat16)
    d_normed_mlp = reduce_sum(jnp.einsum('bsf,hf->bsh', d_pre, w_up, preferred_element_type=jnp.float32).astype(jnp.bfloat16))
    d_w_up = jnp.einsum('bsh,bsf->hf', saved['normed_mlp'], d_pre, preferred_element_type=jnp.float32).astype(jnp.bfloat16)
    _, norm_mlp_back = jax.vjp(layer_norm, saved['resid_f32'], gain_mlp.astype(jnp.float32))
    d_resid_norm, d_gain_mlp = norm_mlp_back(d_normed_mlp.astype(jnp.float32))
    d_resid = (d_out.astype(jnp.float32) + d_resid_norm).astype(jnp.bfloat16)
    d_heads = jnp.einsum('bsh,ndh->bnsd', d_resid, w_out, preferred_element_type=jnp.float32).astype(jnp.bfloat16)
    d_w_out = jnp.einsum('bnsd,bsh->ndh', saved['attn_heads'], d_resid, preferred_element_type=jnp.float32).astype(jnp.bfloat16)
    d_probs = jnp.einsum('bnqd,bnkd->bnqk', d_heads, qkv_all[2], preferred_element_type=jnp.float32)
    d_value = jnp.einsum('bnqk,bnqd->bnkd', saved['probs_bf'], d_heads, preferred_element_type=jnp.float32).astype(jnp.bfloat16)
    row_dot = jnp.sum(d_probs * attn_probs, axis=-1, keepdims=True)
    d_scores = (attn_probs * (d_probs - row_dot) * (head_dim ** -0.5)).astype(jnp.bfloat16)
    d_query = jnp.einsum('bnqk,bnkd->bnqd', d_scores, qkv_all[1], preferred_element_type=jnp.float32).astype(jnp.bfloat16)
    d_key = jnp.einsum('bnqk,bnqd->bnkd', d_scores, qkv_all[0], preferred_element_type=jnp.float32).astype(jnp.bfloat16)
    d_qkv = jnp.stack([d_query, d_key, d_value])
    d_normed = reduce_sum(jnp.einsum('jbnsd,hnjd->bsh', d_qkv, w_qkv, preferred_element_type=jnp.float32).astype(jnp.bfloat16))
    d_w_qkv = jnp.einsum('bsh,jbnsd->hnjd', saved['normed'], d_qkv, preferred_element_type=jnp.float32).astype(jnp.bfloat16)
    _, norm_attn_back = jax.vjp(layer_norm, tokens.astype(jnp.float32), gain_attn.astype(jnp.float32))
    d_x_norm, d_gain_attn = norm_attn_back(d_normed.astype(jnp.float32))
    d_tokens = (d_resid.astype(jnp.float32) + d_x_norm).astype(jnp.bfloat16)
    return (d_tokens, d_w_qkv, d_w_out, d_w_up, d_w_down, d_gain_attn, d_gain_mlp)


def solution(mesh):
    reduce_sum = functools.partial(lax.psum, axis_name='model')

    def device_step(tokens, seg_ids, d_out, gain_attn, gain_mlp, w_qkv, w_out, w_up, w_down):
        allowed = causal_mask(seg_ids)
        layer_out, _ = forward_pass(tokens, allowed, gain_attn, gain_mlp, w_qkv, w_out, w_up, w_down, reduce_sum)
        tokens_again = lax.optimization_barrier((tokens, layer_out))[0]
        _, saved = forward_pass(tokens_again, allowed, gain_attn, gain_mlp, w_qkv, w_out, w_up, w_down, reduce_sum)
        grad_list = backward_pass(tokens_again, d_out, gain_attn, gain_mlp, w_qkv, w_out, w_up, w_down, saved, reduce_sum)
        return (layer_out,) + grad_list

    in_specs = (P('data', None, None), P('data', None), P('data', None, None), P(), P(), P(None, 'model', None, None), P('model', None, None), P(None, 'model'), P('model', None))
    out_specs = (P('data', None, None), P('data', None, None), P('data', 'model', None, None), P(('data', 'model'), None, None), P('data', 'model'), P(('data', 'model'), None), P('data'), P('data'))
    return jax.shard_map(device_step, mesh=mesh, in_specs=in_specs, out_specs=out_specs, check_vma=False)
```

profile of v0, /device:TPU:113, one launch (start us, length us, event | category | flops | bytes accessed | tf_op | source)
XLA Modules:
  0.0 871.0 jit_solution(14030600383927611560)
XLA Ops:
  16.4 16.7 %convert_bitcast_fusion.1 = bf16[3,8,3,192,128]{4,3,0,2,1:T(8,128)(2,1)S(1)} fusion(bf16[8,192,3072]{2,1,0:T(8,128)(2,1)S(1)} %copy-done.1, f32[3072]{0:T(1024)S(1)} %convert_element_type.159, f32[8,192]{1,0:T(8,128)S(1)} %add_rsqrt_fusion.1, f32[8,192]{1,0:T(8,128)S(1)} %broadcast_multiply_fusion.3, bf16[3072,3,3,128]{3,0,2,1:T(8,128)(2,1)} %param.14), kind=kOutput, calls=%fused_computation.128 | convolution fusion | flops 10896998400 | bytes 20078592 | tf_op jit(solution)/shard_map/bsh,hnjd->jbnsd/dot_general | solution.py:29
  38.0 10.2 %bitcast_convert_fusion.2 = bf16[8,192,3072]{2,1,0:T(8,128)(2,1)} fusion(bf16[3,128,3072]{2,1,0:T(8,128)(2,1)S(1)} %copy-done, f32[8,3,192,192]{2,3,1,0:T(8,128)} %get-tuple-element.27, f32[8,3,192]{2,1,0:T(4,128)S(1)} %get-tuple-element.26, bf16[3,8,3,192,128]{4,3,0,2,1:T(8,128)(2,1)} %copy-done.8), kind=kOutput, calls=%fused_computation.55 | convolution fusion | flops 3857448960 | bytes 17713152 | tf_op jit(solution)/shard_map/bnsd,ndh->bsh/dot_general | solution.py:34
  48.9 107.9 %all-reduce.6.cloned.1.call-done = bf16[8,192,3072]{2,1,0:T(8,128)(2,1)} async-done(((bf16[8,192,3072]{2,1,0:T(8,128)(2,1)}), bf16[8,192,3072]{2,1,0:T(8,128)(2,1)}) %all-reduce.6.cloned.1.call-update) | async-done | bytes 9437200 | tf_op jit(solution)/shard_map/psum | solution.py:34
  171.6 28.6 %convolution_convert_fusion.1 = bf16[8,192,3072]{2,1,0:T(8,128)(2,1)} fusion(bf16[1024,3072]{1,0:T(8,128)(2,1)} %param.17, bf16[3072,1024]{1,0:T(8,128)(2,1)} %param.16, bf16[8,192,3072]{2,1,0:T(8,128)(2,1)} %copy-done.3, f32[3072]{0:T(1024)S(1)} %convert_element_type.169, f32[8,192]{1,0:T(8,128)S(1)} %add_rsqrt_fusion, ...), kind=kOutput, calls=%fused_computation.88 | convolution fusion | flops 19369820160 | bytes 31481856 | tf_op jit(solution)/shard_map/bsf,fh->bsh/dot_general | solution.py:39
  200.4 105.6 %all-reduce.8.cloned.1.call-done = bf16[8,192,3072]{2,1,0:T(8,128)(2,1)} async-done(((bf16[8,192,3072]{2,1,0:T(8,128)(2,1)}), bf16[8,192,3072]{2,1,0:T(8,128)(2,1)}) %all-reduce.8.cloned.1.call-update) | async-done | bytes 9437200 | tf_op jit(solution)/shard_map/psum | solution.py:39
  306.0 12.7 %fusion.32 = bf16[8,192,3072]{2,1,0:T(8,128)(2,1)} fusion(bf16[8,192,3072]{2,1,0:T(8,128)(2,1)} %copy-done.3, bf16[8,192,3072]{2,1,0:T(8,128)(2,1)} %all-reduce.8.cloned.1.call-done), kind=kLoop, calls=%fused_computation.49 | loop fusion | flops 18874368 | bytes 28311552 | tf_op jit(solution)/shard_map/convert_element_type | solution.py:40
  330.9 16.1 %convert_bitcast_fusion = bf16[3,8,3,192,128]{4,3,0,2,1:T(8,128)(2,1)S(1)} fusion(f32[3072]{0:T(1024)S(1)} %convert_element_type.159, f32[8,192]{1,0:T(8,128)S(1)} %fusion.166, f32[8,192]{1,0:T(8,128)S(1)} %broadcast_multiply_fusion.1, bf16[8,192,3072]{2,1,0:T(8,128)(2,1)S(1)} %bitcast.141, bf16[3072,3,3,128]{3,0,2,1:T(8,128)(2,1)} %param.14), kind=kOutput, calls=%fused_computation.127 | convolution fusion | flops 10896998400 | bytes 20078592 | tf_op jit(solution)/shard_map/bsh,hnjd->jbnsd/dot_general | solution.py:29
  360.9 105.6 %all-reduce.10.cloned.1.call-done = bf16[8,192,3072]{2,1,0:T(8,128)(2,1)} async-done(((bf16[8,192,3072]{2,1,0:T(8,128)(2,1)}), bf16[8,192,3072]{2,1,0:T(8,128)(2,1)}) %all-reduce.10.cloned.1.call-update) | async-done | bytes 9437200 | tf_op jit(solution)/shard_map/psum | solution.py:34
  478.6 14.4 %fusion.81 = f32[8,192,1024]{2,1,0:T(8,128)} fusion(bf16[3072,1024]{1,0:T(8,128)(2,1)} %param.16, bf16[8,192,3072]{2,1,0:T(8,128)(2,1)S(1)} %get-tuple-element.23, f32[8,192]{1,0:T(8,128)S(1)} %fusion.167, f32[8,192]{1,0:T(8,128)S(1)} %broadcast_multiply_fusion, f32[3072]{0:T(1024)S(1)} %convert_element_type.169), kind=kOutput, calls=%fused_computation.111 | convolution fusion | flops 9687269376 | bytes 22044672 | tf_op jit(solution)/shard_map/bsh,hf->bsf/dot_general | solution.py:37
  493.0 19.9 %fusion.61 = bf16[8,192,1024]{2,1,0:T(8,128)(2,1)} fusion(f32[8,192,1024]{2,1,0:T(8,128)} %fusion.81, bf16[8,192,3072]{2,1,0:T(8,128)(2,1)} %param.11, bf16[1024,3072]{1,0:T(8,128)(2,1)} %param.17), kind=kOutput, calls=%fused_computation.91 | convolution fusion | flops 9698279424 | bytes 25165824 | tf_op jit(solution)/shard_map/bsh,fh->bsf/dot_general | solution.py:49
  512.9 14.3 %convolution_convert_fusion = bf16[8,192,3072]{2,1,0:T(8,128)(2,1)} fusion(bf16[8,192,1024]{2,1,0:T(8,128)(2,1)} %fusion.61, bf16[3072,1024]{1,0:T(8,128)(2,1)S(1)} %bitcast.149), kind=kOutput, calls=%fused_computation.87 | convolution fusion | flops 9668395008 | bytes 18874368 | tf_op jit(solution)/shard_map/bsf,hf->bsh/dot_general | solution.py:53
  527.4 16.6 %bitcast_convert_fusion.5 = bf16[3072,1024]{1,0:T(8,128)(2,1)} fusion(bf16[8,192,1024]{2,1,0:T(8,128)(2,1)} %fusion.61, bf16[8,192,3072]{2,1,0:T(8,128)(2,1)} %copy-done.2, f32[8,192]{1,0:T(8,128)S(1)} %fusion.167, f32[8,192]{1,0:T(8,128)S(1)} %broadcast_multiply_fusion, f32[3072]{0:T(1024)S(1)} %convert_element_type.169), kind=kOutput, calls=%fused_computation.60 | convolution fusion | flops 9690415104 | bytes 18898944 | tf_op jit(solution)/shard_map/bsh,bsf->hf/dot_general | solution.py:54
  543.9 89.0 %all-reduce.12.cloned.1.call-done = bf16[8,192,3072]{2,1,0:T(8,128)(2,1)} async-done(((bf16[8,192,3072]{2,1,0:T(8,128)(2,1)}), bf16[8,192,3072]{2,1,0:T(8,128)(2,1)}) %all-reduce.12.cloned.1.call-update) | async-done | bytes 9437200 | tf_op jit(solution)/shard_map/psum | solution.py:53
  633.0 10.3 %fusion.28 = f32[8,192]{1,0:T(8,128)S(1)} fusion(bf16[8,192,3072]{2,1,0:T(8,128)(2,1)} %all-reduce.12.cloned.1.call-done, bf16[8,192,3072]{2,1,0:T(8,128)(2,1)} %copy-done.2, f32[8,192]{1,0:T(8,128)S(1)} %broadcast_multiply_fusion, f32[3072]{0:T(1024)S(1)} %convert_element_type.169), kind=kLoop, calls=%fused_computation.45 | loop fusion | flops 28310016 | bytes 18898944 | tf_op jit(solution)/shard_map/transpose(jvp())/reduce_sum | solution.py:14
  643.3 14.4 %fusion.29 = (f32[3072]{0:T(1024)}, f32[8,192]{1,0:T(8,128)S(1)}) fusion(bf16[8,192,3072]{2,1,0:T(8,128)(2,1)} %all-reduce.12.cloned.1.call-done, bf16[8,192,3072]{2,1,0:T(8,128)(2,1)} %copy-done.2, f32[8,192]{1,0:T(8,128)S(1)} %fusion.167, f32[8,192]{1,0:T(8,128)S(1)} %broadcast_multiply_fusion, f32[8,192]{1,0:T(8,128)S(1)} %multiply_multiply_fusion.4, ...), kind=kLoop, calls=%fused_computation.46 | loop fusion | flops 56618496 | bytes 18923520 | tf_op jit(solution)/shard_map/transpose(jvp())/reduce_sum | solution.py:14
  657.8 13.6 %add_convert_fusion.1 = bf16[8,192,3072]{2,1,0:T(8,128)(2,1)S(1)} fusion(bf16[8,192,3072]{2,1,0:T(8,128)(2,1)} %param.11, bf16[8,192,3072]{2,1,0:T(8,128)(2,1)S(1)} %bitcast.147, bf16[8,192,3072]{2,1,0:T(8,128)(2,1)S(1)} %copy-done.5, f32[8,192]{1,0:T(8,128)S(1)} %negate_multiply_fusion.1, f32[8,192]{1,0:T(8,128)S(1)} %multiply_multiply_fusion.4, ...), kind=kLoop, calls=%fused_computation.57 | loop fusion | flops 56623104 | bytes 37785600 | tf_op jit(solution)/shard_map/convert_element_type | solution.py:57
  701.7 18.0 %bitcast_convert_fusion = bf16[8,192,3072]{2,1,0:T(8,128)(2,1)} fusion(bf16[1,8,3,192,128]{4,3,2,1,0:T(8,128)(2,1)S(1)} %fusion.149, bf16[1,8,3,192,128]{4,3,2,1,0:T(8,128)(2,1)} %fusion.150, bf16[1,8,3,192,128]{4,3,2,1,0:T(8,128)(2,1)} %fusion.153, bf16[3072,3,3,128]{3,0,2,1:T(8,128)(2,1)} %param.14), kind=kOutput, calls=%fused_computation.53 | convolution fusion | flops 10879893504 | bytes 20054016 | tf_op jit(solution)/shard_map/jbnsd,hnjd->bsh/dot_general | solution.py:67
  719.9 17.7 %bitcast_convert_fusion.4 = bf16[1024,3072]{1,0:T(8,128)(2,1)} fusion(bf16[8,192,3072]{2,1,0:T(8,128)(2,1)} %param.11, f32[8,192,1024]{2,1,0:T(8,128)} %fusion.81), kind=kOutput, calls=%fused_computation.59 | convolution fusion | flops 9680977920 | bytes 22020096 | tf_op jit(solution)/shard_map/bsf,bsh->fh/dot_general | solution.py:50
  737.7 15.1 %fusion.57 = bf16[3072,3,3,128]{0,3,1,2:T(8,128)(2,1)} fusion(f32[3072]{0:T(1024)S(1)} %copy-done.12, f32[8,192]{1,0:T(8,128)S(1)} %copy-done.14, f32[8,192]{1,0:T(8,128)S(1)} %copy-done.10, bf16[8,192,3072]{2,1,0:T(8,128)(2,1)S(1)} %bitcast.143, bf16[1,8,3,192,128]{4,3,2,1,0:T(8,128)(2,1)S(1)} %copy-done.23, ...), kind=kOutput, calls=%fused_computation.85 | convolution fusion | flops 10902306816 | bytes 20078592 | tf_op jit(solution)/shard_map/bsh,jbnsd->hnjd/dot_general | solution.py:68
  752.7 10.5 %copy.23 = bf16[3072,3,3,128]{3,0,2,1:T(8,128)(2,1)} copy(bf16[3072,3,3,128]{0,3,1,2:T(8,128)(2,1)} %fusion.57) | data formatting | bytes 14155776
  772.6 52.9 %all-reduce.14.cloned.1.call-done = bf16[8,192,3072]{2,1,0:T(8,128)(2,1)} async-done(((bf16[8,192,3072]{2,1,0:T(8,128)(2,1)}), bf16[8,192,3072]{2,1,0:T(8,128)(2,1)}) %all-reduce.14.cloned.1.call-update) | async-done | bytes 9437200 | tf_op jit(solution)/shard_map/psum | solution.py:67
  825.5 10.3 %fusion.34 = f32[8,192]{1,0:T(8,128)S(1)} fusion(bf16[8,192,3072]{2,1,0:T(8,128)(2,1)} %all-reduce.14.cloned.1.call-done, bf16[8,192,3072]{2,1,0:T(8,128)(2,1)} %param.9, f32[8,192]{1,0:T(8,128)S(1)} %copy-done.10, f32[3072]{0:T(1024)S(1)} %copy-done.12), kind=kLoop, calls=%fused_computation.51 | loop fusion | flops 28310016 | bytes 18898944 | tf_op jit(solution)/shard_map/transpose(jvp())/reduce_sum | solution.py:14
  835.8 13.9 %fusion.30 = (f32[3072]{0:T(1024)}, f32[8,192]{1,0:T(8,128)S(1)}) fusion(bf16[8,192,3072]{2,1,0:T(8,128)(2,1)} %all-reduce.14.cloned.1.call-done, bf16[8,192,3072]{2,1,0:T(8,128)(2,1)} %param.9, f32[8,192]{1,0:T(8,128)S(1)} %copy-done.14, f32[8,192]{1,0:T(8,128)S(1)} %copy-done.10, f32[8,192]{1,0:T(8,128)S(1)} %multiply_multiply_fusion.3, f32[3072]{0:T(1024)S(1)} %copy-done.12), kind=kLoop, calls=%fused_computation.47 | loop fusion | flops 56618496 | bytes 18923520 | tf_op jit(solution)/shard_map/transpose(jvp())/reduce_sum | solution.py:14
  849.8 14.4 %add_convert_fusion = bf16[8,192,3072]{2,1,0:T(8,128)(2,1)} fusion(bf16[8,192,3072]{2,1,0:T(8,128)(2,1)} %copy-done.6, bf16[8,192,3072]{2,1,0:T(8,128)(2,1)S(1)} %bitcast.145, bf16[8,192,3072]{2,1,0:T(8,128)(2,1)S(1)} %copy-done.4, f32[8,192]{1,0:T(8,128)S(1)} %negate_multiply_fusion, f32[8,192]{1,0:T(8,128)S(1)} %multiply_multiply_fusion.3, ...), kind=kLoop, calls=%fused_computation.56 | loop fusion | flops 56623104 | bytes 37785600 | tf_op jit(solution)/shard_map/convert_element_type | solution.py:71
  (140 shorter events, 107.4 us)
Async XLA Ops:
  7.2 30.8 %copy-start = (bf16[3,128,3072]{2,1,0:T(8,128)(2,1)S(1)}, bf16[3,128,3072]{2,1,0:T(8,128)(2,1)}, u32[]{:S(2)}) copy-start(bf16[3,128,3072]{2,1,0:T(8,128)(2,1)} %param.15) | copy-start | bytes 7077892
  7.2 149.6 %all-reduce.6.cloned.1.call-start = ((), (), s32[]{:S(2)}) async-start(), calls=%async_computation | async-start | bytes 18874368 | tf_op jit(solution)/shard_map/psum | solution.py:34
  16.4 313.8 %copy-start.11 = (f32[3072]{0:T(1024)}, f32[3072]{0:T(1024)S(1)}, u32[]{:S(2)}) copy-start(f32[3072]{0:T(1024)S(1)} %convert_element_type.159) | copy-start | bytes 36868
  48.3 257.7 %all-reduce.8.cloned.1.call-start = ((), (), s32[]{:S(2)}) async-start(), calls=%async_computation.1 | async-start | bytes 18874368 | tf_op jit(solution)/shard_map/psum | solution.py:39
  200.3 266.2 %all-reduce.10.cloned.1.call-start = ((), (), s32[]{:S(2)}) async-start(), calls=%async_computation.2 | async-start | bytes 18874368 | tf_op jit(solution)/shard_map/psum | solution.py:34
  323.9 23.2 %copy-start.9 = (f32[8,192]{1,0:T(8,128)}, f32[8,192]{1,0:T(8,128)S(1)}, u32[]{:S(2)}) copy-start(f32[8,192]{1,0:T(8,128)S(1)} %broadcast_multiply_fusion.1) | copy-start | bytes 18436
  330.2 16.8 %copy-start.15 = (f32[8,192]{1,0:T(8,128)}, f32[8,192]{1,0:T(8,128)S(1)}, u32[]{:S(2)}) copy-start(f32[8,192]{1,0:T(8,128)S(1)} %fusion.33) | copy-start | bytes 18436
  360.8 272.2 %all-reduce.12.cloned.1.call-start = ((), (), s32[]{:S(2)}) async-start(), calls=%async_computation.3 | async-start | bytes 18874368 | tf_op jit(solution)/shard_map/psum | solution.py:53
  478.6 34.4 %slice-start.12 = ((s8[6291456]{0:T(1024)(128)(4,1)}), s8[2097152]{0:T(1024)(128)(4,1)S(1)}, s32[]{:S(2)}) async-start(s8[6291456]{0:T(1024)(128)(4,1)} %bitcast.148), calls=%async_computation.17 | async-start | bytes 4194304
  493.0 20.0 %slice-start.13 = ((s8[6291456]{0:T(1024)(128)(4,1)}), s8[4194304]{0:T(1024)(128)(4,1)S(1)}, s32[]{:S(2)}) async-start(s8[6291456]{0:T(1024)(128)(4,1)} %bitcast.148), calls=%async_computation.18 | async-start | bytes 8388608
  527.3 298.2 %all-reduce.14.cloned.1.call-start = ((), (), s32[]{:S(2)}) async-start(), calls=%async_computation.4 | async-start | bytes 18874368 | tf_op jit(solution)/shard_map/psum | solution.py:67
  643.3 33.4 %slice-start.14 = ((s8[4718592]{0:T(1024)(128)(4,1)}), s8[4194304]{0:T(1024)(128)(4,1)S(1)}, s32[]{:S(2)}) async-start(s8[4718592]{0:T(1024)(128)(4,1)} %bitcast.150), calls=%async_computation.19 | async-start | bytes 8388608
  657.8 18.9 %slice-start.15 = ((s8[4718592]{0:T(1024)(128)(4,1)}), s8[524288]{0:T(1024)(128)(4,1)S(1)}, s32[]{:S(2)}) async-start(s8[4718592]{0:T(1024)(128)(4,1)} %bitcast.150), calls=%async_computation.20 | async-start | bytes 1048576
  677.5 24.2 %copy-start.22 = (bf16[1,8,3,192,128]{4,3,2,1,0:T(8,128)(2,1)}, bf16[1,8,3,192,128]{4,3,2,1,0:T(8,128)(2,1)S(1)}, u32[]{:S(2)}) copy-start(bf16[1,8,3,192,128]{4,3,2,1,0:T(8,128)(2,1)S(1)} %fusion.149) | copy-start | bytes 3538948
  719.7 17.9 %slice-start.3 = ((s8[9437184]{0:T(1024)(128)(4,1)}), s8[1048576]{0:T(1024)(128)(4,1)S(1)}, s32[]{:S(2)}) async-start(s8[9437184]{0:T(1024)(128)(4,1)} %bitcast.142), calls=%async_computation.8 | async-start | bytes 2097152
  719.8 17.8 %slice-start.4 = ((s8[9437184]{0:T(1024)(128)(4,1)}), s8[4194304]{0:T(1024)(128)(4,1)S(1)}, s32[]{:S(2)}) async-start(s8[9437184]{0:T(1024)(128)(4,1)} %bitcast.142), calls=%async_computation.9 | async-start | bytes 8388608
  719.8 17.8 %slice-start.5 = ((s8[9437184]{0:T(1024)(128)(4,1)}), s8[4194304]{0:T(1024)(128)(4,1)S(1)}, s32[]{:S(2)}) async-start(s8[9437184]{0:T(1024)(128)(4,1)} %bitcast.142), calls=%async_computation.10 | async-start | bytes 8388608
  719.8 17.8 %copy-start.10 = (f32[8,192]{1,0:T(8,128)S(1)}, f32[8,192]{1,0:T(8,128)}, u32[]{:S(2)}) copy-start(f32[8,192]{1,0:T(8,128)} %copy-done.9) | copy-start | bytes 18436
  719.8 17.8 %copy-start.12 = (f32[3072]{0:T(1024)S(1)}, f32[3072]{0:T(1024)}, u32[]{:S(2)}) copy-start(f32[3072]{0:T(1024)} %copy-done.11) | copy-start | bytes 36868
  719.8 17.8 %copy-start.14 = (f32[8,192]{1,0:T(8,128)S(1)}, f32[8,192]{1,0:T(8,128)}, u32[]{:S(2)}) copy-start(f32[8,192]{1,0:T(8,128)} %copy-done.13) | copy-start | bytes 18436
  719.8 17.8 %copy-start.23 = (bf16[1,8,3,192,128]{4,3,2,1,0:T(8,128)(2,1)S(1)}, bf16[1,8,3,192,128]{4,3,2,1,0:T(8,128)(2,1)}, u32[]{:S(2)}) copy-start(bf16[1,8,3,192,128]{4,3,2,1,0:T(8,128)(2,1)} %copy-done.22) | copy-start | bytes 3538948
  719.8 17.8 %copy-start.26 = (bf16[1,8,3,192,128]{4,3,2,1,0:T(8,128)(2,1)S(1)}, bf16[1,8,3,192,128]{4,3,2,1,0:T(8,128)(2,1)}, u32[]{:S(2)}) copy-start(bf16[1,8,3,192,128]{4,3,2,1,0:T(8,128)(2,1)} %fusion.153) | copy-start | bytes 3538948
  719.9 17.8 %copy-start.27 = (bf16[1,8,3,192,128]{4,3,2,1,0:T(8,128)(2,1)S(1)}, bf16[1,8,3,192,128]{4,3,2,1,0:T(8,128)(2,1)}, u32[]{:S(2)}) copy-start(bf16[1,8,3,192,128]{4,3,2,1,0:T(8,128)(2,1)} %fusion.150) | copy-start | bytes 3538948
  772.6 63.2 %copy-start.16 = (f32[8,192]{1,0:T(8,128)S(1)}, f32[8,192]{1,0:T(8,128)}, u32[]{:S(2)}) copy-start(f32[8,192]{1,0:T(8,128)} %copy-done.15) | copy-start | bytes 18436
  (25 other events, 189.0 us)
Sparse Core Ops, SparseCore 0:
  48.4 108.3 all-reduce.5
  200.4 105.5 all-reduce.7
  360.9 105.5 all-reduce.9
  527.4 105.5 all-reduce.11
  719.9 105.5 all-reduce.13
where the time goes:
time: 875 us; the launch traced here: 871 us
  waiting for transfers between devices  461 us (53%)
  matrix products  237 us (27%)
  other arithmetic  137 us (16%)
  local copies, waits for them, and re-layouts  20.1 us (2%)
  between operations  14.8 us (2%)
    psum x2, waiting for transfers between devices, forward_pass(): reduce_sum(jnp.einsum('bnsd,ndh->bsh', attn_heads, w_out, preferred_eleme...  213 us
    psum x1, waiting for transfers between devices, forward_pass(): reduce_sum(jnp.einsum('bsf,fh->bsh', hidden, w_down, preferred_element_ty...  106 us
    psum x1, waiting for transfers between devices, backward_pass(): reduce_sum(jnp.einsum('bsf,hf->bsh', d_pre, w_up, preferred_element_type=...  89 us
    psum x1, waiting for transfers between devices, backward_pass(): reduce_sum(jnp.einsum('jbnsd,hnjd->bsh', d_qkv, w_qkv, preferred_element_...  52.9 us
    reduce_sum x4, other arithmetic, layer_norm(): return centered * lax.rsqrt(var_val + NORM_EPS) * gain_vec  48.9 us
    dot_general x2, matrix products, forward_pass(): jnp.einsum('bsh,hnjd->jbnsd', normed, w_qkv, preferred_element_type=jnp.f...  32.8 us
    dot_general x1, matrix products, forward_pass(): jnp.einsum('bsf,fh->bsh', hidden, w_down, preferred_element_type=jnp.floa...  28.6 us
    reduce_sum x4, other arithmetic, layer_norm(): mean_val = jnp.mean(values, axis=-1, keepdims=True)  27 us
  transfers between devices with their start and end apart: 5, of which 5 were waited for; matrix products, arithmetic and copies ran while one was open for 8% of the time, Pallas kernels for 0%

commit v1 on v0

v1 whole, which is shorter than its diff:
```python
import functools
import jax
import jax.numpy as jnp
from jax import lax
from jax.experimental import pallas as pl
from jax.experimental.pallas import tpu as pltpu
from jax.sharding import PartitionSpec as P

NORM_EPS = 1e-5
AXIS = 'model'
F32 = jnp.float32
BF16 = jnp.bfloat16
VMEM_BYTES = 62 * 2 ** 20

MESH = pl.DeviceIdType.MESH
STEP = 48
NORM_STEP = 96
SPLIT = 2
KINDS = 18


class Ring:
    def __init__(self, part, out, own, swp, mid_a, mid_b, fin_p, fin_m, rows, load_sem, send, recv, store_sem):
        self.part, self.out, self.own, self.swp = part, out, own, swp
        self.mid_a, self.mid_b, self.fin_p, self.fin_m, self.rows = mid_a, mid_b, fin_p, fin_m, rows
        self.load_sem, self.send, self.recv, self.store_sem = load_sem, send, recv, store_sem
        me = lax.axis_index('model')
        chips = lax.axis_size('model') // 2
        chip, core = me // 2, lax.rem(me, 2)
        self.me = me
        self.peer = 2 * chip + 1 - core
        self.plus = 2 * lax.rem(chip + 1, chips) + core
        self.minus = 2 * lax.rem(chip + chips - 1, chips) + core
        self.far = 2 * lax.rem(chip + 2, chips) + core
        self.seq_len = part.shape[1]
        self.piece = self.seq_len // SPLIT
        self.half = self.piece // 2

    def barrier(self, everyone):
        sem = pltpu.get_barrier_semaphore()
        count = lax.axis_size('model')
        near = (self.peer, self.plus, self.minus)
        devices = [lax.rem(self.me + r, count) for r in range(1, count)] if everyone else near
        for dev in devices:
            pl.semaphore_signal(sem, inc=1, device_id={'model': dev}, device_id_type=MESH)
        pl.semaphore_wait(sem, len(devices))

    def rcopy(self, h, kind, src, dst, dev):
        return pltpu.make_async_remote_copy(src_ref=src, dst_ref=dst, send_sem=self.send.at[h, kind],
                                            recv_sem=self.recv.at[h, kind], device_id={'model': dev}, device_id_type=MESH)

    def p(self, h): return pl.ds(h * self.piece, self.piece)
    def a(self, h): return pl.ds(h * self.piece, self.half)
    def b(self, h): return pl.ds(h * self.piece + self.half, self.half)

    def targets(self):
        return (self.far, self.plus, self.minus, self.me)

    def swap_copy(self, h, j):
        blk = self.targets()[j]
        other = blk + 1 - 2 * lax.rem(blk, 2)
        return self.rcopy(h, j, self.part.at[other, self.p(h)], self.swp.at[j, self.p(h)], self.peer)

    def load_copy(self, h, j):
        return pltpu.make_async_copy(self.part.at[self.targets()[j], self.p(h)], self.own.at[j, self.p(h)], self.load_sem.at[h, j])

    def c4(self, h): return self.rcopy(h, 4, self.own.at[0, self.a(h)], self.mid_a.at[h], self.plus)
    def c5(self, h): return self.rcopy(h, 5, self.own.at[0, self.b(h)], self.mid_b.at[h], self.minus)
    def c6(self, h): return self.rcopy(h, 6, self.own.at[1, self.b(h)], self.fin_p.at[self.b(h)], self.plus)
    def c7(self, h): return self.rcopy(h, 7, self.own.at[2, self.a(h)], self.fin_m.at[self.a(h)], self.minus)
    def c8(self, h): return self.rcopy(h, 8, self.own.at[1, self.a(h)], self.fin_p.at[self.a(h)], self.plus)
    def c9(self, h): return self.rcopy(h, 9, self.own.at[2, self.b(h)], self.fin_m.at[self.b(h)], self.minus)
    def c10(self, h): return self.rcopy(h, 10, self.rows.at[self.p(h)], self.out.at[self.me, self.p(h)], self.plus)
    def c11(self, h): return self.rcopy(h, 11, self.rows.at[self.p(h)], self.out.at[self.me, self.p(h)], self.minus)
    def c12(self, h): return self.rcopy(h, 12, self.rows.at[self.p(h)], self.out.at[self.me, self.p(h)], self.peer)
    def c13(self, h): return self.rcopy(h, 13, self.out.at[self.minus, self.a(h)], self.out.at[self.minus, self.a(h)], self.plus)
    def c14(self, h): return self.rcopy(h, 14, self.out.at[self.plus, self.b(h)], self.out.at[self.plus, self.b(h)], self.minus)
    def c15(self, h): return self.rcopy(h, 15, self.out.at[self.minus, self.p(h)], self.out.at[self.minus, self.p(h)], self.peer)
    def c16(self, h): return self.rcopy(h, 16, self.out.at[self.plus, self.p(h)], self.out.at[self.plus, self.p(h)], self.peer)
    def c17(self, h): return self.rcopy(h, 17, self.out.at[self.far, self.p(h)], self.out.at[self.far, self.p(h)], self.peer)
    def keep(self, h): return pltpu.make_async_copy(self.rows.at[self.p(h)], self.out.at[self.me, self.p(h)], self.store_sem.at[h])

    def begin(self, everyone=False):
        for h in range(SPLIT):
            for j in range(4):
                self.load_copy(h, j).start()
        self.barrier(everyone)
        for h in range(SPLIT):
            for j in range(4):
                self.swap_copy(h, j).start()

    def add(self, j, row0, count, src, src_row0):
        def body(i, carry):
            at = pl.ds(pl.multiple_of(row0 + i * STEP, STEP), STEP)
            fr = pl.ds(pl.multiple_of(src_row0 + i * STEP, STEP), STEP)
            self.own[j, at] = (self.own[j, at].astype(jnp.float32) + src[fr].astype(jnp.float32)).astype(jnp.bfloat16)
            return carry
        lax.fori_loop(0, count // STEP, body, 0)

    def merge_swap(self, h, j):
        self.load_copy(h, j).wait()
        self.swap_copy(h, j).wait_recv()
        self.add(j, h * self.piece, self.piece, self.swp.at[j], h * self.piece)

    def first(self, h):
        self.merge_swap(h, 0)
        self.c4(h).start()
        self.c5(h).start()
        self.merge_swap(h, 1)
        self.c6(h).start()
        self.merge_swap(h, 2)
        self.c7(h).start()

    def second(self, h):
        self.c4(h).wait_recv()
        self.add(1, h * self.piece, self.half, self.mid_a.at[h], 0)
        self.c8(h).start()
        self.c5(h).wait_recv()
        self.add(2, h * self.piece + self.half, self.half, self.mid_b.at[h], 0)
        self.c9(h).start()

    def finish(self, h, middle):
        self.load_copy(h, 3).wait()
        self.swap_copy(h, 3).wait_recv()
        self.c6(h).wait_recv()
        self.c8(h).wait_recv()
        self.c7(h).wait_recv()
        self.c9(h).wait_recv()

        def body(i, carry):
            at = pl.ds(pl.multiple_of(h * self.piece + i * STEP, STEP), STEP)
            f = lambda r: r.astype(jnp.float32)
            total = (f(self.own[3, at]) + f(self.swp[3, at])) + (f(self.fin_p[at]) + f(self.fin_m[at]))
            return middle(at, total, carry)
        return lax.fori_loop(0, self.piece // STEP, body, 0)

    def share(self, h):
        self.keep(h).start()
        self.c10(h).start()
        self.c11(h).start()
        self.c12(h).start()

    def forward(self, h):
        self.c10(h).wait_recv()
        self.c13(h).start()
        self.c15(h).start()
        self.c11(h).wait_recv()
        self.c14(h).start()
        self.c16(h).start()

    def last(self, h):
        self.c13(h).wait_recv()
        self.c14(h).wait_recv()
        self.c17(h).start()

    def end(self):
        for h in range(SPLIT):
            for c in (self.c12, self.c15, self.c16, self.c17):
                c(h).wait_recv()
            for j in range(4):
                self.swap_copy(h, j).wait_send()
            for c in (self.c4, self.c5, self.c6, self.c7, self.c8, self.c9, self.c10, self.c11, self.c12, self.c13, self.c14, self.c15, self.c16, self.c17):
                c(h).wait_send()
            self.keep(h).wait()


def ring_scratch(seq_len, hidden):
    bf = jnp.bfloat16
    return [pltpu.VMEM((4, seq_len, hidden), bf), pltpu.VMEM((4, seq_len, hidden), bf),
            pltpu.VMEM((SPLIT, seq_len // SPLIT // 2, hidden), bf), pltpu.VMEM((SPLIT, seq_len // SPLIT // 2, hidden), bf),
            pltpu.VMEM((seq_len, hidden), bf), pltpu.VMEM((seq_len, hidden), bf), pltpu.VMEM((seq_len, hidden), bf),
            pltpu.SemaphoreType.DMA((SPLIT, 4)), pltpu.SemaphoreType.DMA((SPLIT, KINDS)), pltpu.SemaphoreType.DMA((SPLIT, KINDS)),
            pltpu.SemaphoreType.DMA((SPLIT,))]


def any_spec():
    return pl.BlockSpec(memory_space=pl.ANY)


def dot_nn(lhs, rhs):
    return lax.dot_general(lhs, rhs, (((1,), (0,)), ((), ())), preferred_element_type=F32)


def dot_nt(lhs, rhs):
    return lax.dot_general(lhs, rhs, (((1,), (1,)), ((), ())), preferred_element_type=F32)


def dot_tn(lhs, rhs):
    return lax.dot_general(lhs, rhs, (((0,), (0,)), ((), ())), preferred_element_type=F32)


def norm_stats(values):
    mean_val = jnp.mean(values, axis=-1, keepdims=True)
    centered = values - mean_val
    var_val = jnp.mean(centered * centered, axis=-1, keepdims=True)
    return centered, lax.rsqrt(var_val + NORM_EPS)


def norm_back(values, gain, grad):
    centered, scale = norm_stats(values)
    unit = centered * scale
    d_unit = grad * gain
    mean_d = jnp.mean(d_unit, axis=-1, keepdims=True)
    mean_du = jnp.mean(d_unit * unit, axis=-1, keepdims=True)
    return scale * (d_unit - mean_d - unit * mean_du), grad * unit


def softmax_of(q, k, keep):
    scores = dot_nt(q, k) * (q.shape[-1] ** -0.5)
    scores = jnp.where(keep > 0.5, scores, -1e30)
    top = jnp.max(scores, axis=-1, keepdims=True)
    weights = jnp.exp(scores - top)
    return weights / jnp.sum(weights, axis=-1, keepdims=True)


def columns_dot(dot, out, lhs, rhs_of, width):
    for c in range(out.shape[-1] // width):
        out[:, c * width:(c + 1) * width] = dot(lhs, rhs_of(c * width, width)).astype(BF16)


def attention_seq(x, a, qkv, o, p1, keep, gain, wq, wo):
    def norm_step(i, carry):
        at = pl.ds(pl.multiple_of(i * NORM_STEP, NORM_STEP), NORM_STEP)
        centered, scale = norm_stats(x[at].astype(F32))
        a[at] = (centered * scale * gain[...]).astype(BF16)
        return carry
    lax.fori_loop(0, x.shape[0] // NORM_STEP, norm_step, 0)
    dim = 128
    for n in range(o.shape[-1] // dim):
        lo = 3 * n * dim
        qkv[:, lo:lo + 3 * dim] = dot_nn(a[...], wq[:, lo:lo + 3 * dim]).astype(BF16)
        q, k, v = (qkv[:, lo + j * dim:lo + (j + 1) * dim] for j in range(3))
        probs = softmax_of(q, k, keep[...]).astype(BF16)
        o[:, n * dim:(n + 1) * dim] = dot_nn(probs, v).astype(BF16)
    columns_dot(dot_nn, p1, o[...], lambda c, w: wo[:, c:c + w], 768)


def attention_back_seq(d_x1, qkv, keep, wq, wo, d_qkv, d_a):
    heads_width = wo.shape[0]
    dim = 128
    d_heads = dot_nt(d_x1[...], wo[...]).astype(BF16)
    for n in range(heads_width // dim):
        lo = 3 * n * dim
        q, k, v = (qkv[:, lo + j * dim:lo + (j + 1) * dim] for j in range(3))
        d_o = d_heads[:, n * dim:(n + 1) * dim]
        probs = softmax_of(q, k, keep[...])
        d_probs = dot_nt(d_o, v)
        row_dot = jnp.sum(d_probs * probs, axis=-1, keepdims=True)
        d_scores = (probs * (d_probs - row_dot) * (dim ** -0.5)).astype(BF16)
        d_qkv[:, lo:lo + dim] = dot_nn(d_scores, k).astype(BF16)
        d_qkv[:, lo + dim:lo + 2 * dim] = dot_tn(d_scores, q).astype(BF16)
        d_qkv[:, lo + 2 * dim:lo + 3 * dim] = dot_tn(probs.astype(BF16), d_o).astype(BF16)
    columns_dot(dot_nt, d_a, d_qkv[...], lambda c, w: wq[c:c + w, :], 512)


def load_wq(wq_hbm, wq, sems):
    dim = wq_hbm.shape[-1]
    return [pltpu.make_async_copy(wq_hbm.at[i], wq.at[:, pl.ds(i * dim, dim)], sems.at[i]) for i in range(wq_hbm.shape[0])]


class Stream:
    def __init__(self, count, in_pairs, out_pairs, in_sem, out_sem):
        self.count, self.in_pairs, self.out_pairs, self.in_sem, self.out_sem = count, in_pairs, out_pairs, in_sem, out_sem

    def loads(self, i, slot):
        return [pltpu.make_async_copy(a, b, self.in_sem.at[k, slot]) for k, (a, b) in enumerate(self.in_pairs(i, slot))]

    def stores(self, i, slot):
        return [pltpu.make_async_copy(a, b, self.out_sem.at[k, slot]) for k, (a, b) in enumerate(self.out_pairs(i, slot))]

    def begin(self):
        for c in self.loads(0, 0):
            c.start()

    def run(self, lo, hi, body):
        def step(i, carry):
            slot = lax.rem(i, 2)
            for c in self.loads(i, slot):
                c.wait()

            @pl.when(i + 1 < self.count)
            def _():
                for c in self.loads(i + 1, 1 - slot):
                    c.start()

            @pl.when(i >= 2)
            def _():
                for c in self.stores(i - 2, slot):
                    c.wait()
            body(slot)
            for c in self.stores(i, slot):
                c.start()
            return carry
        lax.fori_loop(lo, hi, step, 0)

    def end(self):
        for i in (self.count - 2, self.count - 1):
            for c in self.stores(i, i % 2):
                c.wait()


def ring_params(cid):
    return pltpu.CompilerParams(collective_id=cid, has_side_effects=True, vmem_limit_bytes=VMEM_BYTES)


def sds(shape, dtype=BF16):
    return jax.ShapeDtypeStruct(shape, dtype)


def first_kernel(x, keep, gain, wq_hbm, wo, p1, wq, a, qkv, o, sems):
    @pl.when(pl.program_id(0) == 0)
    def _():
        copies = load_wq(wq_hbm, wq, sems)
        for c in copies:
            c.start()
        for c in copies:
            c.wait()
    attention_seq(x.at[0], a, qkv, o, p1.at[0], keep.at[0], gain, wq, wo)


def first_call(tokens, keep, gain, wq, wo):
    seqs, seq_len, hidden = tokens.shape
    width = wq.shape[0] * wq.shape[2]
    seq = lambda w: pl.BlockSpec((1, seq_len, w), lambda i: (i, 0, 0))
    return pl.pallas_call(
        first_kernel, grid=(seqs,), out_shape=sds(tokens.shape),
        in_specs=[seq(hidden), seq(seq_len), pl.BlockSpec(gain.shape, lambda i: (0, 0)), any_spec(), pl.BlockSpec(wo.shape, lambda i: (0, 0))],
        out_specs=seq(hidden),
        scratch_shapes=[pltpu.VMEM((hidden, width), BF16), pltpu.VMEM((seq_len, hidden), BF16), pltpu.VMEM((seq_len, width), BF16),
                        pltpu.VMEM((seq_len, wo.shape[0]), BF16), pltpu.SemaphoreType.DMA((wq.shape[0],))],
        compiler_params=pltpu.CompilerParams(vmem_limit_bytes=VMEM_BYTES),
        cost_estimate=pl.CostEstimate(flops=20 * 10 ** 9, bytes_accessed=30 * 10 ** 6, transcendentals=0))(tokens, keep, gain, wq, wo)


def residual_events(ring, x_rows, x1_rows, gain):
    def middle(at, total, carry):
        x1 = (x_rows[at].astype(F32) + total.astype(BF16).astype(F32)).astype(BF16)
        x1_rows[at] = x1
        centered, scale = norm_stats(x1.astype(F32))
        ring.rows[at] = (centered * scale * gain[...]).astype(BF16)
        return carry
    return ring_events(ring, middle)


def ring_events(ring, middle):
    events = [functools.partial(ring.first, h) for h in range(SPLIT)]
    events += [functools.partial(ring.second, h) for h in range(SPLIT)]

    def close(h):
        ring.finish(h, middle)
        ring.share(h)
    events += [functools.partial(close, h) for h in range(SPLIT)]
    events += [functools.partial(ring.forward, h) for h in range(SPLIT)]
    events += [functools.partial(ring.last, h) for h in range(SPLIT)]
    return events


def interleave(events, tasks, counts):
    pending = [[run, 0, total] for total, run in tasks]
    for event, n in zip(events, counts):
        while n and pending:
            run, lo, total = pending[0]
            hi = min(lo + n, total)
            run(lo, hi)
            n -= hi - lo
            pending[0][1] = hi
            if hi == total:
                pending.pop(0)
        event()
    for run, lo, total in pending:
        run(lo, total)


def ka_kernel(p1, tokens, keep, gain_a, gain_m, wq_hbm, wo_hbm,
              b_out, x1_out, a_out, qkv_out, o_out, p1_out,
              x_rows, x1_rows, row_sem, wq, wo, wq_sem, wo_sem, x2, keep2, a2, qkv2, o2, p2, in_sem, out_sem, *ring_scr):
    ring = Ring(p1, b_out, *ring_scr)
    ring.begin()
    loads = [pltpu.make_async_copy(tokens.at[ring.me], x_rows, row_sem.at[0]), pltpu.make_async_copy(wo_hbm, wo, wo_sem)]
    weights = load_wq(wq_hbm, wq, wq_sem)
    stream = Stream(tokens.shape[0], lambda i, t: [(tokens.at[i], x2.at[t]), (keep.at[i], keep2.at[t])],
                    lambda i, t: [(a2.at[t], a_out.at[i]), (qkv2.at[t], qkv_out.at[i]), (o2.at[t], o_out.at[i]), (p2.at[t], p1_out.at[i])],
                    in_sem, out_sem)
    for c in loads + weights:
        c.start()
    stream.begin()
    for c in loads + weights:
        c.wait()

    def task(lo, hi):
        stream.run(lo, hi, lambda t: attention_seq(x2.at[t], a2.at[t], qkv2.at[t], o2.at[t], p2.at[t], keep2.at[t], gain_a, wq, wo))
    interleave(residual_events(ring, x_rows, x1_rows, gain_m), [(stream.count, task)], PLAN)
    keep_rows = pltpu.make_async_copy(x1_rows, x1_out, row_sem.at[1])
    keep_rows.start()
    stream.end()
    keep_rows.wait()
    ring.end()


PLAN = (0, 0, 1, 2, 2, 1, 1, 1, 0, 0)


def ka_call(p1, tokens, keep, gain_a, gain_m, wq, wo, cid):
    seqs, seq_len, hidden = tokens.shape
    width, inner = wq.shape[0] * wq.shape[2], wo.shape[0]
    vm = pl.BlockSpec(memory_space=pltpu.VMEM)
    two = lambda w, t=BF16: pltpu.VMEM((2, seq_len, w), t)
    full = lambda w: sds((seqs, seq_len, w))
    return pl.pallas_call(
        ka_kernel, out_shape=(full(hidden), sds((seq_len, hidden)), full(hidden), full(width), full(inner), full(hidden)),
        in_specs=[any_spec()] * 3 + [vm, vm] + [any_spec()] * 2, out_specs=(any_spec(),) * 6,
        scratch_shapes=[pltpu.VMEM((seq_len, hidden), BF16), pltpu.VMEM((seq_len, hidden), BF16), pltpu.SemaphoreType.DMA((2,)),
                        pltpu.VMEM((hidden, width), BF16), pltpu.VMEM((inner, hidden), BF16), pltpu.SemaphoreType.DMA((wq.shape[0],)), pltpu.SemaphoreType.DMA,
                        two(hidden), two(seq_len, F32), two(hidden), two(width), two(inner), two(hidden),
                        pltpu.SemaphoreType.DMA((2, 2)), pltpu.SemaphoreType.DMA((4, 2))] + ring_scratch(seq_len, hidden),
        compiler_params=ring_params(cid),
        cost_estimate=pl.CostEstimate(flops=80 * 10 ** 9, bytes_accessed=80 * 10 ** 6, transcendentals=0))(p1, tokens, keep, gain_a, gain_m, wq, wo)


def gelu(values):
    return jax.nn.gelu(values, approximate=True)


def mlp_seq(b, p2, hid, w_up, w_down):
    inner = w_up.shape[1]
    for c in range(0, inner, 256):
        hid[:, c:c + 256] = gelu(dot_nn(b[...], w_up[:, c:c + 256])).astype(BF16)
    columns_dot(dot_nn, p2, hid[...], lambda c, w: w_down[:, c:c + w], 512)


def kb_kernel(p1, tokens, b_fwd, gain_m, up_hbm, down_hbm, b_out, x1_out, p2_out,
              x_rows, x1_rows, row_sem, w_up, w_down, w_sem, b2, p2, hid, in_sem, out_sem, *ring_scr):
    ring = Ring(p1, b_out, *ring_scr)
    ring.begin()
    loads = [pltpu.make_async_copy(tokens.at[ring.me], x_rows, row_sem.at[0]),
             pltpu.make_async_copy(up_hbm, w_up, w_sem.at[0]), pltpu.make_async_copy(down_hbm, w_down, w_sem.at[1])]
    stream = Stream(b_fwd.shape[0], lambda i, t: [(b_fwd.at[i], b2.at[t])], lambda i, t: [(p2.at[t], p2_out.at[i])], in_sem, out_sem)
    for c in loads:
        c.start()
    stream.begin()
    for c in loads:
        c.wait()

    def task(lo, hi):
        stream.run(lo, hi, lambda t: mlp_seq(b2.at[t], p2.at[t], hid, w_up, w_down))
    interleave(residual_events(ring, x_rows, x1_rows, gain_m), [(stream.count, task)], PLAN)
    keep_rows = pltpu.make_async_copy(x1_rows, x1_out, row_sem.at[1])
    keep_rows.start()
    stream.end()
    keep_rows.wait()
    ring.end()


def kb_call(p1, tokens, b_fwd, gain_m, w_up, w_down, cid):
    seqs, seq_len, hidden = tokens.shape
    inner = w_up.shape[1]
    vm = pl.BlockSpec(memory_space=pltpu.VMEM)
    return pl.pallas_call(
        kb_kernel, out_shape=(sds(tokens.shape), sds((seq_len, hidden)), sds(tokens.shape)),
        in_specs=[any_spec()] * 3 + [vm] + [any_spec()] * 2, out_specs=(any_spec(),) * 3,
        scratch_shapes=[pltpu.VMEM((seq_len, hidden), BF16), pltpu.VMEM((seq_len, hidden), BF16), pltpu.SemaphoreType.DMA((2,)),
                        pltpu.VMEM((hidden, inner), BF16), pltpu.VMEM((inner, hidden), BF16), pltpu.SemaphoreType.DMA((2,)),
                        pltpu.VMEM((2, seq_len, hidden), BF16), pltpu.VMEM((2, seq_len, hidden), BF16), pltpu.VMEM((seq_len, inner), BF16),
                        pltpu.SemaphoreType.DMA((1, 2)), pltpu.SemaphoreType.DMA((1, 2))] + ring_scratch(seq_len, hidden),
        compiler_params=ring_params(cid),
        cost_estimate=pl.CostEstimate(flops=80 * 10 ** 9, bytes_accessed=80 * 10 ** 6, transcendentals=0))(p1, tokens, b_fwd, gain_m, w_up, w_down)


TILE = 384
NARROW = 128
GRAD_PLAN = (0, 0, 2, 4, 4, 2, 2, 2, 0, 0)


def wide_task(lhs_hbm, rhs, out_pairs, l2, g2, sems):
    in_sem, out_sem = sems
    stream = Stream(lhs_hbm.shape[1] // TILE, lambda i, t: [(lhs_hbm.at[:, pl.ds(pl.multiple_of(i * TILE, TILE), TILE)], l2.at[t])], out_pairs, in_sem, out_sem)

    def run(lo, hi):
        stream.run(lo, hi, lambda t: g2.__setitem__(t, dot_tn(l2[t], rhs[...]).astype(BF16)))
    return stream, run


def narrow_task(lhs_hbm, rhs, out_hbm, l2, g2, sems):
    in_sem, out_sem = sems
    span = lambda i: pl.ds(pl.multiple_of(i * NARROW, NARROW), NARROW)
    stream = Stream(lhs_hbm.shape[1] // NARROW, lambda i, t: [(lhs_hbm.at[:, span(i)], l2.at[t])], lambda i, t: [(g2.at[t], out_hbm.at[span(i)])], in_sem, out_sem)

    def run(lo, hi):
        def body(t):
            lhs = l2[t]
            for c in range(0, rhs.shape[1], 1024):
                g2[t, :, c:c + 1024] = dot_tn(lhs, rhs[:, c:c + 1024]).astype(BF16)
        stream.run(lo, hi, body)
    return stream, run


def grad_kernel(last, part, values, resid, gain, wide_l, wide_r, narrow_l, narrow_r, *refs):
    if last:
        other_gain, out, gains_out, wide_out, narrow_out = refs[:5]
        refs = refs[5:]
    else:
        out, gain_out, wide_out, narrow_out = refs[:4]
        refs = refs[4:]
    v_rows, r_rows, row_sem, d_gain, w_r, w_l2, w_g2, n_r, n_l2, n_g2, rhs_sem, w_in, w_outs, n_in, n_outs = refs[:15]
    refs = refs[15:]
    if last:
        g_send, g_recv, g_ssem, g_rsem = refs[:4]
        refs = refs[4:]
    ring = Ring(part, out, *refs)
    ring.begin(everyone=last)
    loads = [pltpu.make_async_copy(values.at[ring.me] if len(values.shape) == 3 else values, v_rows, row_sem.at[0]),
             pltpu.make_async_copy(resid.at[ring.me], r_rows, row_sem.at[1]),
             pltpu.make_async_copy(wide_r, w_r, rhs_sem.at[0]), pltpu.make_async_copy(narrow_r, n_r, rhs_sem.at[1])]
    for c in loads:
        c.start()

    def wide_pairs(i, t):
        at = pl.ds(pl.multiple_of(i * TILE, TILE), TILE)
        if len(wide_out.shape) == 2:
            return [(w_g2.at[t], wide_out.at[at])]
        dim = wide_out.shape[2]
        return [(w_g2.at[t, :, pl.ds(j * dim, dim)], wide_out.at[j, at]) for j in range(wide_out.shape[0])]
    wide, wide_run = wide_task(wide_l, w_r, wide_pairs, w_l2, w_g2, (w_in, w_outs))
    narrow, narrow_run = narrow_task(narrow_l, n_r, narrow_out, n_l2, n_g2, (n_in, n_outs))
    wide.begin()
    narrow.begin()
    for c in loads:
        c.wait()

    d_gain[...] = jnp.zeros_like(d_gain)

    def middle(at, total, carry):
        d_value, d_gain_part = norm_back(v_rows[at].astype(F32), gain[...], total.astype(BF16).astype(F32))
        ring.rows[at] = (r_rows[at].astype(F32) + d_value).astype(BF16)
        d_gain[...] += d_gain_part
        return carry
    events = ring_events(ring, middle)
    hidden = part.shape[2]
    count = lax.axis_size(AXIS)

    def gain_copy(r, sender):
        target = lax.rem(ring.me + r, count)
        return pltpu.make_async_remote_copy(src_ref=g_send, dst_ref=g_recv.at[sender], send_sem=g_ssem.at[r], recv_sem=g_rsem.at[sender],
                                            device_id={AXIS: target}, device_id_type=MESH)

    def gains():
        mine = jnp.sum(d_gain[...], axis=0, keepdims=True)
        if not last:
            gain_out[...] = mine
            return
        g_send[:, :hidden] = mine
        g_send[:, hidden:] = other_gain[...]
        g_recv[ring.me, :, :hidden] = mine
        g_recv[ring.me, :, hidden:] = other_gain[...]
        for r in range(1, count):
            gain_copy(r, ring.me).start()
    events.insert(2 * SPLIT + SPLIT, gains)
    plan = GRAD_PLAN[:3 * SPLIT] + (0,) + GRAD_PLAN[3 * SPLIT:]
    interleave(events, [(wide.count, wide_run), (narrow.count, narrow_run)], plan)
    wide.end()
    narrow.end()
    ring.end()
    if last:
        for r in range(1, count):
            gain_copy(r, lax.rem(ring.me + r, count)).wait_recv()
            gain_copy(r, ring.me).wait_send()
        total = g_recv[0]
        for r in range(1, count):
            total = total + g_recv[r]
        gains_out[...] = total


def grad_call(part, values, resid, gain, wide_l, wide_r, narrow_l, narrow_r, blocks, cid, other_gain=None):
    seqs, seq_len, hidden = part.shape
    last = other_gain is not None
    vm = pl.BlockSpec(memory_space=pltpu.VMEM)
    rows, wide_n, narrow_n = wide_r.shape[0], wide_r.shape[1], narrow_r.shape[1]
    wide_shape = (wide_l.shape[1], wide_n) if blocks == 1 else (blocks, wide_l.shape[1], wide_n // blocks)
    dma = pltpu.SemaphoreType.DMA
    outs = (sds(part.shape), sds((1, 2 * hidden if last else hidden), F32), sds(wide_shape), sds((narrow_l.shape[1], narrow_n)))
    scratch = [pltpu.VMEM((seq_len, hidden), BF16), pltpu.VMEM((seq_len, hidden), BF16), dma((2,)), pltpu.VMEM((STEP, hidden), F32),
               pltpu.VMEM((rows, wide_n), BF16), pltpu.VMEM((2, rows, TILE), BF16), pltpu.VMEM((2, TILE, wide_n), BF16),
               pltpu.VMEM((rows, narrow_n), BF16), pltpu.VMEM((2, rows, NARROW), BF16), pltpu.VMEM((2, NARROW, narrow_n), BF16),
               dma((2,)), dma((1, 2)), dma((blocks, 2)), dma((1, 2)), dma((1, 2))]
    if last:
        count = lax.axis_size(AXIS)
        scratch += [pltpu.VMEM((1, 2 * hidden), F32), pltpu.VMEM((count, 1, 2 * hidden), F32), dma((count,)), dma((count,))]
    args = (part, values, resid, gain, wide_l, wide_r, narrow_l, narrow_r) + ((other_gain,) if last else ())
    return pl.pallas_call(
        functools.partial(grad_kernel, last), out_shape=outs,
        in_specs=[any_spec()] * 3 + [vm] + [any_spec()] * 4 + ([vm] if last else []), out_specs=(any_spec(), vm, any_spec(), any_spec()),
        scratch_shapes=scratch + ring_scratch(seq_len, hidden), compiler_params=ring_params(cid),
        cost_estimate=pl.CostEstimate(flops=80 * 10 ** 9, bytes_accessed=80 * 10 ** 6, transcendentals=0))(*args)


def back_kernel(d_x1, qkv, keep, wq_hbm, wo, d_qkv, d_a, wq, sems):
    @pl.when(pl.program_id(0) == 0)
    def _():
        copies = load_wq(wq_hbm, wq, sems)
        for c in copies:
            c.start()
        for c in copies:
            c.wait()
    attention_back_seq(d_x1.at[0], qkv.at[0], keep.at[0], wq, wo, d_qkv.at[0], d_a.at[0])


def back_call(d_x1, qkv, keep, wq, wo):
    seqs, seq_len, hidden = d_x1.shape
    width = qkv.shape[-1]
    seq = lambda w: pl.BlockSpec((1, seq_len, w), lambda i: (i, 0, 0))
    return pl.pallas_call(
        back_kernel, grid=(seqs,), out_shape=(sds(qkv.shape), sds(d_x1.shape)),
        in_specs=[seq(hidden), seq(width), seq(seq_len), any_spec(), pl.BlockSpec(wo.shape, lambda i: (0, 0))],
        out_specs=(seq(width), seq(hidden)),
        scratch_shapes=[pltpu.VMEM((hidden, width), BF16), pltpu.SemaphoreType.DMA((wq.shape[0],))],
        compiler_params=pltpu.CompilerParams(vmem_limit_bytes=VMEM_BYTES),
        cost_estimate=pl.CostEstimate(flops=20 * 10 ** 9, bytes_accessed=30 * 10 ** 6, transcendentals=0))(d_x1, qkv, keep, wq, wo)


def dot_of(spec, lhs, rhs):
    return jnp.einsum(spec, lhs, rhs, preferred_element_type=F32)


def solution(mesh):
    def device_step(tokens, seg_ids, d_out, gain_attn, gain_mlp, w_qkv, w_out, w_up, w_down):
        seqs, seq_len, hidden = tokens.shape
        row_count = seqs * seq_len
        heads, dim = w_qkv.shape[1], w_qkv.shape[3]
        at_pos = lax.broadcasted_iota(jnp.int32, (seq_len, seq_len), 0) >= lax.broadcasted_iota(jnp.int32, (seq_len, seq_len), 1)
        keep = ((seg_ids[:, :, None] == seg_ids[:, None, :]) & at_pos[None]).astype(F32)
        gain_a = gain_attn.astype(F32)[None]
        gain_m = gain_mlp.astype(F32)[None]
        wq = jnp.transpose(w_qkv, (1, 2, 0, 3)).reshape(heads * 3, hidden, dim)
        wo = w_out.reshape(heads * dim, hidden)
        flat = lambda v: v.reshape(row_count, v.shape[-1])

        p1 = first_call(tokens, keep, gain_a, wq, wo)
        b_full, x1_rows, normed, qkv, heads_out, p1_again = ka_call(p1, tokens, keep, gain_a, gain_m, wq, wo, 0)
        b_again, x1_again, p2 = kb_call(p1_again, tokens, b_full, gain_m, w_up, w_down, 1)
        p2_rows = lax.psum_scatter(flat(p2), AXIS, scatter_dimension=0, tiled=True)
        out_rows = (x1_rows.astype(F32) + p2_rows.astype(F32)).astype(BF16)

        pre_act = dot_of('rh,hf->rf', flat(b_again), w_up)
        hidden_act, gelu_back = jax.vjp(gelu, pre_act)
        hidden_act = hidden_act.astype(BF16)
        d_hidden = dot_of('rh,fh->rf', flat(d_out), w_down).astype(BF16)
        d_pre = gelu_back(d_hidden.astype(F32))[0].astype(BF16)
        d_b = dot_of('rf,hf->rh', d_pre, w_up).astype(BF16).reshape(tokens.shape)
        d_x1, d_gain_m, d_w_up, d_w_down = grad_call(d_b, x1_again, d_out, gain_m, flat(b_again), d_pre, hidden_act, flat(d_out), 1, 2)
        d_x1, out_rows = lax.optimization_barrier((d_x1, out_rows))
        layer_out = lax.all_gather(out_rows, AXIS, axis=0, tiled=True).reshape(tokens.shape)
        d_qkv, d_a = back_call(d_x1, qkv, keep, wq, wo)
        d_tokens, d_gain, d_wq, d_wo = grad_call(d_a, tokens, d_x1, gain_a, flat(normed), flat(d_qkv), flat(heads_out), flat(d_x1), heads * 3, 3, d_gain_m)
        d_w_qkv = jnp.transpose(d_wq.reshape(heads, 3, hidden, dim), (2, 0, 1, 3))
        d_w_out = d_wo.reshape(w_out.shape)
        d_gain_a, d_gain_m = d_gain[0, :hidden], d_gain[0, hidden:]
        return layer_out, d_tokens, d_w_qkv, d_w_out, d_w_up, d_w_down, d_gain_a, d_gain_m

    in_specs = (P('data', None, None), P('data', None), P('data', None, None), P(), P(), P(None, 'model', None, None), P('model', None, None), P(None, 'model'), P('model', None))
    out_specs = (P('data', None, None), P('data', None, None), P('data', 'model', None, None), P(('data', 'model'), None, None), P('data', 'model'), P(('data', 'model'), None), P('data'), P('data'))
    return jax.shard_map(device_step, mesh=mesh, in_specs=in_specs, out_specs=out_specs, check_vma=False)
```

time: 875 us -> 562 us (0.64)
  waiting for transfers between devices: 461 us -> 0.13 us
  Pallas kernels: 0 us -> 445 us
  matrix products: 237 us -> 51.5 us
  other arithmetic: 137 us -> 7.49 us
  local copies, waits for them, and re-layouts: 20.1 us -> 33.5 us
    psum x5 -> x0, waiting for transfers between devices: 461 us -> none  [the longest x2 213 us: forward_pass(): reduce_sum(jnp.einsum('bnsd,ndh->bsh', attn_heads, w_out, preferred_eleme...]
    pallas_call x0 -> x6, Pallas kernels: none -> 445 us  [the longest x2 182 us: grad_call(): pl.pallas_call(functools.partial(grad_kernel, last), out_shape=outs, in_s...]
    dot_general x21 -> x3, matrix products: 237 us -> 51.5 us  [dot_of(): return jnp.einsum(spec, lhs, rhs, preferred_element_type=F32)]
    reduce_sum x12 -> x0, other arithmetic: 90.1 us -> none  [the longest x4 48.9 us: layer_norm(): return centered * lax.rsqrt(var_val + NORM_EPS) * gain_vec]
    convert_element_type x5 -> x2, other arithmetic: 40.8 us -> 4.88 us  [the longest x1 2.69 us: device_step(): out_rows = (x1_rows.astype(F32) + p2_rows.astype(F32)).astype(BF16)]
    unnamed x89 -> x24, local copies, waits for them, and re-layouts: 20.1 us -> 32.1 us
  transfers between devices with their start and end apart: 5 -> 2, of which waited for: 5 -> 0; matrix products, arithmetic and copies ran while one was open for 8% -> 10% of each run, Pallas kernels for 0% -> 41%
where the time goes in v1:
time: 562 us; the launch traced here: 552 us
  Pallas kernels  445 us (79%)
  matrix products  51.5 us (9%)
  local copies, waits for them, and re-layouts  33.5 us (6%)
  between operations  14.6 us (3%)
  other arithmetic  7.49 us (1%)
    pallas_call x2, Pallas kernels, grad_call(): pl.pallas_call(functools.partial(grad_kernel, last), out_shape=outs, in_s...  182 us
    pallas_call x1, Pallas kernels, ka_call(): pl.pallas_call(ka_kernel, out_shape=(full(hidden), sds((seq_len, hidden))...  90.3 us
    pallas_call x1, Pallas kernels, kb_call(): pl.pallas_call(kb_kernel, out_shape=(sds(tokens.shape), sds((seq_len, hid...  88.4 us
    dot_general x3, matrix products, dot_of(): return jnp.einsum(spec, lhs, rhs, preferred_element_type=F32)  51.5 us
    pallas_call x1, Pallas kernels, first_call(): pl.pallas_call(first_kernel, grid=(seqs,), out_shape=sds(tokens.shape), i...  42.1 us
    pallas_call x1, Pallas kernels, back_call(): pl.pallas_call(back_kernel, grid=(seqs,), out_shape=(sds(qkv.shape), sds(...  42.1 us
    unnamed x24, local copies, waits for them, and re-layouts  32.1 us
  transfers between devices with their start and end apart: 2, of which 0 were waited for; matrix products, arithmetic and copies ran while one was open for 10% of the time, Pallas kernels for 41%

profile of v1, /device:TPU:113, one launch (start us, length us, event | category | flops | bytes accessed | tf_op | source)
XLA Modules:
  0.0 552.2 jit_solution(5194846339046676822)
XLA Ops:
  7.2 0.1 reduce-scatter.2.cloned.1.call-start
  7.3 1.3 broadcast_in_dim.17
  8.6 1.3 broadcast_in_dim.18
  9.9 2.2 and_convert_fusion.keep
  12.1 42.1 %shard_map.152.p1 = bf16[8,192,3072]{2,1,0:T(8,128)(2,1)} custom-call(bf16[8,192,3072]{2,1,0:T(8,128)(2,1)} %values.1, f32[8,192,192]{2,1,0:T(8,128)} %and_convert_fusion.keep, f32[1,3072]{1,0:T(1,128)} %bitcast.35, bf16[9,3072,128]{2,1,0:T(8,128)(2,1)} %bitcast.47, bf16[384,3072]{1,0:T(8,128)(2,1)} %bitcast.50), custom_call_target="tpu_custom_call" | custom-call | flops 20000000000 | bytes 30000000 | tf_op jit(solution)/shard_map/pallas_call | solution.py:325
  54.2 90.3 %shard_map.153 = (bf16[8,192,3072]{2,1,0:T(8,128)(2,1)}, bf16[192,3072]{1,0:T(8,128)(2,1)}, bf16[8,192,3072]{2,1,0:T(8,128)(2,1)}, bf16[8,192,1152]{2,1,0:T(8,12...) custom-call(bf16[8,192,3072]{2,1,0:T(8,128)(2,1)} %shard_map.152.p1, bf16[8,192,3072]{2,1,0:T(8,128)(2,1)} %values.1, ...), custom_call_target="tpu_custom_call" | custom-call | flops 80000000000 | bytes 80000000 | tf_op jit(solution)/shard_map/pallas_call | solution.py:409
  144.5 88.4 %shard_map.154 = (bf16[8,192,3072]{2,1,0:T(8,128)(2,1)}, bf16[192,3072]{1,0:T(8,128)(2,1)}, bf16[8,192,3072]{2,1,0:T(8,128)(2,1)}) custom-call(bf16[8,192,3072]{2,1,0:T(8,128)(2,1)} %get-tuple-element.29.p1, bf16[8,192,3072]{2,1,0:T(8,128)(2,1)} %values.1, bf16[8,192,3072]{2,1,0:T(8,128)(2,1)} %get-tuple-element.30.b_fwd, f32[1,3072]{1,0:T(1,128)} %bitcast.39, ...), custom_call_target="tpu_custom_call" | custom-call | flops 80000000000 | bytes 80000000 | tf_op jit(solution)/shard_map/pallas_call | solution.py:458
  233.0 0.1 all-gather.2.cloned.1.call-start
  233.1 18.1 %multiply_convert_fusion = (bf16[1536,1024]{1,0:T(8,128)(2,1)}, f32[1536,1024]{1,0:T(8,128)}) fusion(bf16[1536,3072]{1,0:T(8,128)(2,1)} %bitcast.55, bf16[3072,1024]{1,0:T(8,128)(2,1)} %up_hbm.1), kind=kOutput, calls=%fused_computation.15 | convolution fusion | flops 9677832192 | bytes 25165824 | tf_op jit(solution)/shard_map/rh,hf->rf/dot_general | solution.py:621
  251.3 17.9 %fusion.2.wide_r = bf16[1536,1024]{1,0:T(8,128)(2,1)} fusion(f32[1536,1024]{1,0:T(8,128)} %get-tuple-element.53, bf16[1536,3072]{1,0:T(8,128)(2,1)S(1)} %bitcast.46, bf16[1024,3072]{1,0:T(8,128)(2,1)} %down_hbm.1), kind=kOutput, calls=%fused_computation.7 | convolution fusion | flops 9698279424 | bytes 25165824 | tf_op jit(solution)/shard_map/rh,fh->rf/dot_general | solution.py:621
  269.3 15.4 %convolution_convert_fusion = bf16[1536,3072]{1,0:T(8,128)(2,1)} fusion(bf16[1536,1024]{1,0:T(8,128)(2,1)} %fusion.2.wide_r, bf16[3072,1024]{1,0:T(8,128)(2,1)} %up_hbm.1), kind=kOutput, calls=%fused_computation | convolution fusion | flops 9668395008 | bytes 18874368 | tf_op jit(solution)/shard_map/rf,hf->rh/dot_general | solution.py:621
  284.7 89.8 %shard_map.155 = (bf16[8,192,3072]{2,1,0:T(8,128)(2,1)}, f32[1,3072]{1,0:T(1,128)}, bf16[3072,1024]{1,0:T(8,128)(2,1)}, bf16[1024,3072]{1,0:T(8,128)(2,1)}) custom-call(bf16[8,192,3072]{2,1,0:T(8,128)(2,1)} %bitcast.57, bf16[192,3072]{1,0:T(8,128)(2,1)} %get-tuple-element.32.values, bf16[8,192,3072]{2,1,0:T(8,128)(2,1)} %resid.1, f32[1,3072]{1,0:T(1,128)} %bitcast.40, ...), custom_call_target="tpu_custom_call" | custom-call | flops 80000000000 | bytes 80000000 | tf_op jit(solution)/shard_map/pallas_call | solution.py:589
  374.5 2.7 add_convert_fusion
  377.3 42.1 %shard_map.156 = (bf16[8,192,1152]{2,1,0:T(8,128)(2,1)}, bf16[8,192,3072]{2,1,0:T(8,128)(2,1)}) custom-call(bf16[8,192,3072]{2,1,0:T(8,128)(2,1)} %get-tuple-element.37.d_x1.resid, bf16[8,192,1152]{2,1,0:T(8,128)(2,1)} %get-tuple-element.38.qkv, f32[8,192,192]{2,1,0:T(8,128)} %and_convert_fusion.keep, bf16[9,3072,128]{2,1,0:T(8,128)(2,1)} %bitcast.49, ...), custom_call_target="tpu_custom_call" | custom-call | flops 20000000000 | bytes 30000000 | tf_op jit(solution)/shard_map/pallas_call | solution.py:611
  419.4 92.1 %shard_map.157 = (bf16[8,192,3072]{2,1,0:T(8,128)(2,1)}, f32[1,6144]{1,0:T(1,128)}, bf16[9,3072,128]{2,1,0:T(8,128)(2,1)}, bf16[384,3072]{1,0:T(8,128)(2,1)}) custom-call(bf16[8,192,3072]{2,1,0:T(8,128)(2,1)} %get-tuple-element.39.part, bf16[8,192,3072]{2,1,0:T(8,128)(2,1)} %values.1, bf16[8,192,3072]{2,1,0:T(8,128)(2,1)} %get-tuple-element.37.d_x1.resid, ...), custom_call_target="tpu_custom_call" | custom-call | flops 80000000000 | bytes 80000000 | tf_op jit(solution)/shard_map/pallas_call | solution.py:589
  511.5 1.3 fusion.10
  512.8 8.3 %copy.23 = bf16[8,192,3072]{2,1,0:T(8,128)(2,1)} copy(bf16[8,192,3072]{2,1,0:T(8,128)(2,1)} %bitcast.27) | data formatting | bytes 18874368
  521.1 8.4 %copy.24 = bf16[8,192,3072]{2,1,0:T(8,128)(2,1)} copy(bf16[8,192,3072]{2,1,0:T(8,128)(2,1)} %get-tuple-element.63) | data formatting | bytes 18874368
  529.5 6.6 %copy.25 = bf16[3072,3,3,128]{3,0,2,1:T(8,128)(2,1)} copy(bf16[3072,3,3,128]{3,0,2,1:T(8,128)(2,1)} %bitcast.29) | data formatting | bytes 14155776
  536.1 1.4 copy.26
  537.5 3.2 copy.27
  540.7 0.1 slice-done
  540.8 1.4 slice-done.1
  542.2 2.7 copy.28
  (24 shorter events, 0.2 us)
Async XLA Ops:
  7.2 367.3 %reduce-scatter.2.cloned.1.call-start = ((), (), s32[]{:S(2)}) async-start(), calls=%async_computation.1 | async-start | bytes 10616832 | tf_op jit(solution)/shard_map/reduce_scatter | solution.py:640
  233.0 18.3 %slice-start.4 = ((s8[9437184]{0:T(1024)(128)(4,1)}), s8[1048576]{0:T(1024)(128)(4,1)S(1)}, s32[]{:S(2)}) async-start(s8[9437184]{0:T(1024)(128)(4,1)} %bitcast.44), calls=%async_computation.7 | async-start | bytes 2097152
  233.0 279.8 %all-gather.2.cloned.1.call-start = ((), (), s32[]{:S(2)}) async-start(), calls=%async_computation.2 | async-start | bytes 10616832 | tf_op jit(solution)/shard_map/all_gather | solution.py:651
  233.1 18.2 %slice-start.5 = ((s8[9437184]{0:T(1024)(128)(4,1)}), s8[4194304]{0:T(1024)(128)(4,1)S(1)}, s32[]{:S(2)}) async-start(s8[9437184]{0:T(1024)(128)(4,1)} %bitcast.44), calls=%async_computation.8 | async-start | bytes 8388608
  233.1 18.2 %slice-start.6 = ((s8[9437184]{0:T(1024)(128)(4,1)}), s8[4194304]{0:T(1024)(128)(4,1)S(1)}, s32[]{:S(2)}) async-start(s8[9437184]{0:T(1024)(128)(4,1)} %bitcast.44), calls=%async_computation.9 | async-start | bytes 8388608
  284.7 89.9 %copy-start.1 = (bf16[192,3072]{1,0:T(8,128)(2,1)S(1)}, bf16[192,3072]{1,0:T(8,128)(2,1)}, u32[]{:S(2)}) copy-start(bf16[192,3072]{1,0:T(8,128)(2,1)} %get-tuple-element.34) | copy-start | bytes 3538948
  521.1 16.4 %slice-start.2 = ((s8[6291456]{0:T(1024)(128)(4,1)}), s8[2097152]{0:T(1024)(128)(4,1)S(1)}, s32[]{:S(2)}) async-start(s8[6291456]{0:T(1024)(128)(4,1)} %bitcast.32), calls=%async_computation.5 | async-start | bytes 4194304
  529.5 6.6 %copy-start = (bf16[384,3072]{1,0:T(8,128)(2,1)S(1)}, bf16[384,3072]{1,0:T(8,128)(2,1)}, u32[]{:S(2)}) copy-start(bf16[384,3072]{1,0:T(8,128)(2,1)} %get-tuple-element.46) | copy-start | bytes 7077892
  529.5 8.0 %slice-start.3 = ((s8[6291456]{0:T(1024)(128)(4,1)}), s8[4194304]{0:T(1024)(128)(4,1)S(1)}, s32[]{:S(2)}) async-start(s8[6291456]{0:T(1024)(128)(4,1)} %bitcast.32), calls=%async_computation.6 | async-start | bytes 8388608
  536.1 4.7 slice-start
  537.5 4.7 slice-start.1
Sparse Core Ops, SparseCore 0:
  233.2 53.0 reduce-scatter.1
  377.4 50.5 all-gather.1

commit v2 on v1

--- a/solution.py
+++ b/solution.py
@@ -20,19 +20,19 @@
 
 
 class Ring:
-    def __init__(self, part, out, own, swp, mid_a, mid_b, fin_p, fin_m, rows, load_sem, send, recv, store_sem):
-        self.part, self.out, self.own, self.swp = part, out, own, swp
+    def __init__(self, part, out, own, swp, mid_a, mid_b, fin_p, fin_m, rows, load_sem, send, recv, store_sem, give=None):
+        self.part, self.out, self.own, self.swp, self.give = part, out, own, swp, give
         self.mid_a, self.mid_b, self.fin_p, self.fin_m, self.rows = mid_a, mid_b, fin_p, fin_m, rows
         self.load_sem, self.send, self.recv, self.store_sem = load_sem, send, recv, store_sem
         me = lax.axis_index('model')
         chips = lax.axis_size('model') // 2
         chip, core = me // 2, lax.rem(me, 2)
-        self.me = me
+        self.me, self.chip, self.chips, self.core = me, chip, chips, core
         self.peer = 2 * chip + 1 - core
         self.plus = 2 * lax.rem(chip + 1, chips) + core
         self.minus = 2 * lax.rem(chip + chips - 1, chips) + core
         self.far = 2 * lax.rem(chip + 2, chips) + core
-        self.seq_len = part.shape[1]
+        self.seq_len = out.shape[1]
         self.piece = self.seq_len // SPLIT
         self.half = self.piece // 2
 
@@ -57,9 +57,21 @@
         return (self.far, self.plus, self.minus, self.me)
 
     def swap_copy(self, h, j):
+        if self.give is not None:
+            return self.rcopy(h, j, self.give.at[j, self.p(h)], self.swp.at[j, self.p(h)], self.peer)
         blk = self.targets()[j]
         other = blk + 1 - 2 * lax.rem(blk, 2)
         return self.rcopy(h, j, self.part.at[other, self.p(h)], self.swp.at[j, self.p(h)], self.peer)
+
+    def produce_order(self, i):
+        j, mine = i // 2, i % 2
+        offset = 2 - j + 3 * (j // 2) + 2 * (j // 3)
+        side = self.core * mine + (1 - self.core) * (1 - mine)
+        return 2 * lax.rem(self.chip + offset, self.chips) + side
+
+    def swap(self, j):
+        for h in range(SPLIT):
+            self.swap_copy(h, j).start()
 
     def load_copy(self, h, j):
         return pltpu.make_async_copy(self.part.at[self.targets()[j], self.p(h)], self.own.at[j, self.p(h)], self.load_sem.at[h, j])
@@ -81,6 +93,9 @@
     def keep(self, h): return pltpu.make_async_copy(self.rows.at[self.p(h)], self.out.at[self.me, self.p(h)], self.store_sem.at[h])
 
     def begin(self, everyone=False):
+        if self.give is not None:
+            self.barrier(everyone)
+            return
         for h in range(SPLIT):
             for j in range(4):
                 self.load_copy(h, j).start()
@@ -98,29 +113,46 @@
         lax.fori_loop(0, count // STEP, body, 0)
 
     def merge_swap(self, h, j):
-        self.load_copy(h, j).wait()
+        if self.give is None:
+            self.load_copy(h, j).wait()
         self.swap_copy(h, j).wait_recv()
         self.add(j, h * self.piece, self.piece, self.swp.at[j], h * self.piece)
 
-    def first(self, h):
+    def far_side(self, h):
         self.merge_swap(h, 0)
         self.c4(h).start()
         self.c5(h).start()
+
+    def plus_direct(self, h):
         self.merge_swap(h, 1)
         self.c6(h).start()
+
+    def minus_direct(self, h):
         self.merge_swap(h, 2)
         self.c7(h).start()
 
-    def second(self, h):
+    def plus_sum(self, h):
         self.c4(h).wait_recv()
         self.add(1, h * self.piece, self.half, self.mid_a.at[h], 0)
         self.c8(h).start()
+
+    def minus_sum(self, h):
         self.c5(h).wait_recv()
         self.add(2, h * self.piece + self.half, self.half, self.mid_b.at[h], 0)
         self.c9(h).start()
 
+    def first(self, h):
+        self.far_side(h)
+        self.plus_direct(h)
+        self.minus_direct(h)
+
+    def second(self, h):
+        self.plus_sum(h)
+        self.minus_sum(h)
+
     def finish(self, h, middle):
-        self.load_copy(h, 3).wait()
+        if self.give is None:
+            self.load_copy(h, 3).wait()
         self.swap_copy(h, 3).wait_recv()
         self.c6(h).wait_recv()
         self.c8(h).wait_recv()
@@ -222,7 +254,7 @@
     def norm_step(i, carry):
         at = pl.ds(pl.multiple_of(i * NORM_STEP, NORM_STEP), NORM_STEP)
         centered, scale = norm_stats(x[at].astype(F32))
-        a[at] = (centered * scale * gain[...]).astype(BF16)
+        a[at] = (centered * scale * gain[...].astype(F32)).astype(BF16)
         return carry
     lax.fori_loop(0, x.shape[0] // NORM_STEP, norm_step, 0)
     dim = 128
@@ -258,6 +290,15 @@
     return [pltpu.make_async_copy(wq_hbm.at[i], wq.at[:, pl.ds(i * dim, dim)], sems.at[i]) for i in range(wq_hbm.shape[0])]
 
 
+class Once:
+    def __init__(self, copies):
+        self.copies = list(copies)
+
+    def __call__(self):
+        while self.copies:
+            self.copies.pop().wait()
+
+
 class Stream:
     def __init__(self, count, in_pairs, out_pairs, in_sem, out_sem):
         self.count, self.in_pairs, self.out_pairs, self.in_sem, self.out_sem = count, in_pairs, out_pairs, in_sem, out_sem
@@ -307,46 +348,24 @@
     return jax.ShapeDtypeStruct(shape, dtype)
 
 
-def first_kernel(x, keep, gain, wq_hbm, wo, p1, wq, a, qkv, o, sems):
-    @pl.when(pl.program_id(0) == 0)
-    def _():
-        copies = load_wq(wq_hbm, wq, sems)
-        for c in copies:
-            c.start()
-        for c in copies:
-            c.wait()
-    attention_seq(x.at[0], a, qkv, o, p1.at[0], keep.at[0], gain, wq, wo)
-
-
-def first_call(tokens, keep, gain, wq, wo):
-    seqs, seq_len, hidden = tokens.shape
-    width = wq.shape[0] * wq.shape[2]
-    seq = lambda w: pl.BlockSpec((1, seq_len, w), lambda i: (i, 0, 0))
-    return pl.pallas_call(
-        first_kernel, grid=(seqs,), out_shape=sds(tokens.shape),
-        in_specs=[seq(hidden), seq(seq_len), pl.BlockSpec(gain.shape, lambda i: (0, 0)), any_spec(), pl.BlockSpec(wo.shape, lambda i: (0, 0))],
-        out_specs=seq(hidden),
-        scratch_shapes=[pltpu.VMEM((hidden, width), BF16), pltpu.VMEM((seq_len, hidden), BF16), pltpu.VMEM((seq_len, width), BF16),
-                        pltpu.VMEM((seq_len, wo.shape[0]), BF16), pltpu.SemaphoreType.DMA((wq.shape[0],))],
-        compiler_params=pltpu.CompilerParams(vmem_limit_bytes=VMEM_BYTES),
-        cost_estimate=pl.CostEstimate(flops=20 * 10 ** 9, bytes_accessed=30 * 10 ** 6, transcendentals=0))(tokens, keep, gain, wq, wo)
-
-
-def residual_events(ring, x_rows, x1_rows, gain):
+def residual_events(ring, x_rows, x1_rows, gain, ready):
     def middle(at, total, carry):
         x1 = (x_rows[at].astype(F32) + total.astype(BF16).astype(F32)).astype(BF16)
         x1_rows[at] = x1
         centered, scale = norm_stats(x1.astype(F32))
-        ring.rows[at] = (centered * scale * gain[...]).astype(BF16)
+        ring.rows[at] = (centered * scale * gain[...].astype(F32)).astype(BF16)
         return carry
-    return ring_events(ring, middle)
-
-
-def ring_events(ring, middle):
-    events = [functools.partial(ring.first, h) for h in range(SPLIT)]
-    events += [functools.partial(ring.second, h) for h in range(SPLIT)]
+    return ring_events(ring, middle, ready)
+
+
+def ring_events(ring, middle, ready):
+    events = []
+    if ring.give is None:
+        events += [functools.partial(ring.first, h) for h in range(SPLIT)]
+        events += [functools.partial(ring.second, h) for h in range(SPLIT)]
 
     def close(h):
+        ready()
         ring.finish(h, middle)
         ring.share(h)
     events += [functools.partial(close, h) for h in range(SPLIT)]
@@ -371,36 +390,63 @@
         run(lo, total)
 
 
-def ka_kernel(p1, tokens, keep, gain_a, gain_m, wq_hbm, wo_hbm,
+def ka_kernel(tokens, keep, gain_a, gain_m, wq_hbm, wo_hbm,
               b_out, x1_out, a_out, qkv_out, o_out, p1_out,
-              x_rows, x1_rows, row_sem, wq, wo, wq_sem, wo_sem, x2, keep2, a2, qkv2, o2, p2, in_sem, out_sem, *ring_scr):
-    ring = Ring(p1, b_out, *ring_scr)
-    ring.begin()
+              x_rows, x1_rows, row_sem, wq, wo, wq_sem, wo_sem, x2, keep2, a2, qkv2, o2, p2, in_sem, out_sem,
+              give, fx2, fkeep2, f_sem, *ring_scr):
+    ring = Ring(None, b_out, *ring_scr, give=give)
     loads = [pltpu.make_async_copy(tokens.at[ring.me], x_rows, row_sem.at[0]), pltpu.make_async_copy(wo_hbm, wo, wo_sem)]
     weights = load_wq(wq_hbm, wq, wq_sem)
-    stream = Stream(tokens.shape[0], lambda i, t: [(tokens.at[i], x2.at[t]), (keep.at[i], keep2.at[t])],
-                    lambda i, t: [(a2.at[t], a_out.at[i]), (qkv2.at[t], qkv_out.at[i]), (o2.at[t], o_out.at[i]), (p2.at[t], p1_out.at[i])],
-                    in_sem, out_sem)
-    for c in loads + weights:
+    again = Stream(tokens.shape[0], lambda i, t: [(tokens.at[i], x2.at[t]), (keep.at[i], keep2.at[t])],
+                   lambda i, t: [(a2.at[t], a_out.at[i]), (qkv2.at[t], qkv_out.at[i]), (o2.at[t], o_out.at[i]), (p2.at[t], p1_out.at[i])],
+                   in_sem, out_sem)
+    once = Stream(tokens.shape[0], lambda i, t: [(tokens.at[ring.produce_order(i)], fx2.at[t]), (keep.at[ring.produce_order(i)], fkeep2.at[t])],
+                  lambda i, t: [], f_sem, None)
+    once.begin()
+    for c in weights + loads:
         c.start()
-    stream.begin()
-    for c in loads + weights:
-        c.wait()
+    ring.begin()
+    again.begin()
+    ready = Once(weights + loads)
+    ready()
 
     def task(lo, hi):
-        stream.run(lo, hi, lambda t: attention_seq(x2.at[t], a2.at[t], qkv2.at[t], o2.at[t], p2.at[t], keep2.at[t], gain_a, wq, wo))
-    interleave(residual_events(ring, x_rows, x1_rows, gain_m), [(stream.count, task)], PLAN)
+        again.run(lo, hi, lambda t: attention_seq(x2.at[t], a2.at[t], qkv2.at[t], o2.at[t], p2.at[t], keep2.at[t], gain_a, wq, wo))
+
+    def produce(j):
+        for mine, target in enumerate((give, ring.own)):
+            once.run(2 * j + mine, 2 * j + mine + 1, lambda t: attention_seq(
+                fx2.at[t], a2.at[t], qkv2.at[t], o2.at[t], target.at[j], fkeep2.at[t], gain_a, wq, wo))
+            if not mine:
+                ring.swap(j)
+    pieces = range(SPLIT)
+    produce(0)
+    for h in pieces:
+        ring.far_side(h)
+    produce(1)
+    for h in pieces:
+        ring.plus_direct(h)
+    for h in pieces:
+        ring.plus_sum(h)
+    produce(2)
+    for h in pieces:
+        ring.minus_direct(h)
+    for h in pieces:
+        ring.minus_sum(h)
+    produce(3)
+    interleave(residual_events(ring, x_rows, x1_rows, gain_m, ready), [(again.count, task)], KA_PLAN)
     keep_rows = pltpu.make_async_copy(x1_rows, x1_out, row_sem.at[1])
     keep_rows.start()
-    stream.end()
+    again.end()
     keep_rows.wait()
     ring.end()
 
 
-PLAN = (0, 0, 1, 2, 2, 1, 1, 1, 0, 0)
-
-
-def ka_call(p1, tokens, keep, gain_a, gain_m, wq, wo, cid):
+KA_PLAN = (1, 1, 2, 2, 2, 0)
+PLAN = (0, 0, 1, 1, 2, 1, 2, 1, 0, 0)
+
+
+def ka_call(tokens, keep, gain_a, gain_m, wq, wo, cid):
     seqs, seq_len, hidden = tokens.shape
     width, inner = wq.shape[0] * wq.shape[2], wo.shape[0]
     vm = pl.BlockSpec(memory_space=pltpu.VMEM)
@@ -408,42 +454,45 @@
     full = lambda w: sds((seqs, seq_len, w))
     return pl.pallas_call(
         ka_kernel, out_shape=(full(hidden), sds((seq_len, hidden)), full(hidden), full(width), full(inner), full(hidden)),
-        in_specs=[any_spec()] * 3 + [vm, vm] + [any_spec()] * 2, out_specs=(any_spec(),) * 6,
+        in_specs=[any_spec()] * 2 + [vm, vm] + [any_spec()] * 2, out_specs=(any_spec(),) * 6,
         scratch_shapes=[pltpu.VMEM((seq_len, hidden), BF16), pltpu.VMEM((seq_len, hidden), BF16), pltpu.SemaphoreType.DMA((2,)),
                         pltpu.VMEM((hidden, width), BF16), pltpu.VMEM((inner, hidden), BF16), pltpu.SemaphoreType.DMA((wq.shape[0],)), pltpu.SemaphoreType.DMA,
                         two(hidden), two(seq_len, F32), two(hidden), two(width), two(inner), two(hidden),
-                        pltpu.SemaphoreType.DMA((2, 2)), pltpu.SemaphoreType.DMA((4, 2))] + ring_scratch(seq_len, hidden),
+                        pltpu.SemaphoreType.DMA((2, 2)), pltpu.SemaphoreType.DMA((4, 2)),
+                        pltpu.VMEM((4, seq_len, hidden), BF16), two(hidden), two(seq_len, F32), pltpu.SemaphoreType.DMA((2, 2))] + ring_scratch(seq_len, hidden),
         compiler_params=ring_params(cid),
-        cost_estimate=pl.CostEstimate(flops=80 * 10 ** 9, bytes_accessed=80 * 10 ** 6, transcendentals=0))(p1, tokens, keep, gain_a, gain_m, wq, wo)
+        cost_estimate=pl.CostEstimate(flops=80 * 10 ** 9, bytes_accessed=80 * 10 ** 6, transcendentals=0))(tokens, keep, gain_a, gain_m, wq, wo)
 
 
 def gelu(values):
     return jax.nn.gelu(values, approximate=True)
 
 
-def mlp_seq(b, p2, hid, w_up, w_down):
+def mlp_seq(b, d_out, p2, d_hid, hid, w_up, w_down):
     inner = w_up.shape[1]
     for c in range(0, inner, 256):
         hid[:, c:c + 256] = gelu(dot_nn(b[...], w_up[:, c:c + 256])).astype(BF16)
     columns_dot(dot_nn, p2, hid[...], lambda c, w: w_down[:, c:c + w], 512)
-
-
-def kb_kernel(p1, tokens, b_fwd, gain_m, up_hbm, down_hbm, b_out, x1_out, p2_out,
-              x_rows, x1_rows, row_sem, w_up, w_down, w_sem, b2, p2, hid, in_sem, out_sem, *ring_scr):
+    columns_dot(dot_nt, d_hid, d_out[...], lambda c, w: w_down[c:c + w, :], 256)
+
+
+def kb_kernel(p1, tokens, b_fwd, d_out, gain_m, up_hbm, down_hbm, b_out, x1_out, p2_out, dh_out,
+              x_rows, x1_rows, row_sem, w_up, w_down, w_sem, b2, d2, p2, dh2, hid, in_sem, out_sem, *ring_scr):
     ring = Ring(p1, b_out, *ring_scr)
     ring.begin()
     loads = [pltpu.make_async_copy(tokens.at[ring.me], x_rows, row_sem.at[0]),
              pltpu.make_async_copy(up_hbm, w_up, w_sem.at[0]), pltpu.make_async_copy(down_hbm, w_down, w_sem.at[1])]
-    stream = Stream(b_fwd.shape[0], lambda i, t: [(b_fwd.at[i], b2.at[t])], lambda i, t: [(p2.at[t], p2_out.at[i])], in_sem, out_sem)
+    stream = Stream(b_fwd.shape[0], lambda i, t: [(b_fwd.at[i], b2.at[t]), (d_out.at[i], d2.at[t])],
+                    lambda i, t: [(p2.at[t], p2_out.at[i]), (dh2.at[t], dh_out.at[i])], in_sem, out_sem)
     for c in loads:
         c.start()
     stream.begin()
-    for c in loads:
-        c.wait()
+    ready = Once(loads)
 
     def task(lo, hi):
-        stream.run(lo, hi, lambda t: mlp_seq(b2.at[t], p2.at[t], hid, w_up, w_down))
-    interleave(residual_events(ring, x_rows, x1_rows, gain_m), [(stream.count, task)], PLAN)
+        ready()
+        stream.run(lo, hi, lambda t: mlp_seq(b2.at[t], d2.at[t], p2.at[t], dh2.at[t], hid, w_up, w_down))
+    interleave(residual_events(ring, x_rows, x1_rows, gain_m, ready), [(stream.count, task)], PLAN)
     keep_rows = pltpu.make_async_copy(x1_rows, x1_out, row_sem.at[1])
     keep_rows.start()
     stream.end()
@@ -451,19 +500,20 @@
     ring.end()
 
 
-def kb_call(p1, tokens, b_fwd, gain_m, w_up, w_down, cid):
+def kb_call(p1, tokens, b_fwd, d_out, gain_m, w_up, w_down, cid):
     seqs, seq_len, hidden = tokens.shape
     inner = w_up.shape[1]
     vm = pl.BlockSpec(memory_space=pltpu.VMEM)
     return pl.pallas_call(
-        kb_kernel, out_shape=(sds(tokens.shape), sds((seq_len, hidden)), sds(tokens.shape)),
-        in_specs=[any_spec()] * 3 + [vm] + [any_spec()] * 2, out_specs=(any_spec(),) * 3,
+        kb_kernel, out_shape=(sds(tokens.shape), sds((seq_len, hidden)), sds(tokens.shape), sds((seqs, seq_len, inner))),
+        in_specs=[any_spec()] * 4 + [vm] + [any_spec()] * 2, out_specs=(any_spec(),) * 4,
         scratch_shapes=[pltpu.VMEM((seq_len, hidden), BF16), pltpu.VMEM((seq_len, hidden), BF16), pltpu.SemaphoreType.DMA((2,)),
                         pltpu.VMEM((hidden, inner), BF16), pltpu.VMEM((inner, hidden), BF16), pltpu.SemaphoreType.DMA((2,)),
-                        pltpu.VMEM((2, seq_len, hidden), BF16), pltpu.VMEM((2, seq_len, hidden), BF16), pltpu.VMEM((seq_len, inner), BF16),
-                        pltpu.SemaphoreType.DMA((1, 2)), pltpu.SemaphoreType.DMA((1, 2))] + ring_scratch(seq_len, hidden),
+                        pltpu.VMEM((2, seq_len, hidden), BF16), pltpu.VMEM((2, seq_len, hidden), BF16), pltpu.VMEM((2, seq_len, hidden), BF16),
+                        pltpu.VMEM((2, seq_len, inner), BF16), pltpu.VMEM((seq_len, inner), BF16),
+                        pltpu.SemaphoreType.DMA((2, 2)), pltpu.SemaphoreType.DMA((2, 2))] + ring_scratch(seq_len, hidden),
         compiler_params=ring_params(cid),
-        cost_estimate=pl.CostEstimate(flops=80 * 10 ** 9, bytes_accessed=80 * 10 ** 6, transcendentals=0))(p1, tokens, b_fwd, gain_m, w_up, w_down)
+        cost_estimate=pl.CostEstimate(flops=80 * 10 ** 9, bytes_accessed=80 * 10 ** 6, transcendentals=0))(p1, tokens, b_fwd, d_out, gain_m, w_up, w_down)
 
 
 TILE = 384
@@ -492,6 +542,13 @@
                 g2[t, :, c:c + 1024] = dot_tn(lhs, rhs[:, c:c + 1024]).astype(BF16)
         stream.run(lo, hi, body)
     return stream, run
+
+
+def after(ready, run):
+    def call(lo, hi):
+        ready()
+        run(lo, hi)
+    return call
 
 
 def grad_kernel(last, part, values, resid, gain, wide_l, wide_r, narrow_l, narrow_r, *refs):
@@ -524,17 +581,16 @@
     narrow, narrow_run = narrow_task(narrow_l, n_r, narrow_out, n_l2, n_g2, (n_in, n_outs))
     wide.begin()
     narrow.begin()
-    for c in loads:
-        c.wait()
+    ready = Once(loads)
 
     d_gain[...] = jnp.zeros_like(d_gain)
 
     def middle(at, total, carry):
-        d_value, d_gain_part = norm_back(v_rows[at].astype(F32), gain[...], total.astype(BF16).astype(F32))
+        d_value, d_gain_part = norm_back(v_rows[at].astype(F32), gain[...].astype(F32), total.astype(BF16).astype(F32))
         ring.rows[at] = (r_rows[at].astype(F32) + d_value).astype(BF16)
         d_gain[...] += d_gain_part
         return carry
-    events = ring_events(ring, middle)
+    events = ring_events(ring, middle, ready)
     hidden = part.shape[2]
     count = lax.axis_size(AXIS)
 
@@ -556,7 +612,7 @@
             gain_copy(r, ring.me).start()
     events.insert(2 * SPLIT + SPLIT, gains)
     plan = GRAD_PLAN[:3 * SPLIT] + (0,) + GRAD_PLAN[3 * SPLIT:]
-    interleave(events, [(wide.count, wide_run), (narrow.count, narrow_run)], plan)
+    interleave(events, [(wide.count, after(ready, wide_run)), (narrow.count, after(ready, narrow_run))], plan)
     wide.end()
     narrow.end()
     ring.end()
@@ -593,7 +649,10 @@
         cost_estimate=pl.CostEstimate(flops=80 * 10 ** 9, bytes_accessed=80 * 10 ** 6, transcendentals=0))(*args)
 
 
-def back_kernel(d_x1, qkv, keep, wq_hbm, wo, d_qkv, d_a, wq, sems):
+def back_kernel(d_x1, qkv, keep, wq_hbm, wo, g_up, g_down, d_qkv, d_a, up_out, down_out, wq, sems):
+    up_out[...] = g_up[...]
+    down_out[...] = g_down[...]
+
     @pl.when(pl.program_id(0) == 0)
     def _():
         copies = load_wq(wq_hbm, wq, sems)
@@ -604,17 +663,37 @@
     attention_back_seq(d_x1.at[0], qkv.at[0], keep.at[0], wq, wo, d_qkv.at[0], d_a.at[0])
 
 
-def back_call(d_x1, qkv, keep, wq, wo):
+def back_call(d_x1, qkv, keep, wq, wo, g_up, g_down):
     seqs, seq_len, hidden = d_x1.shape
     width = qkv.shape[-1]
+    part = lambda g: pl.BlockSpec((g.shape[0] // seqs, g.shape[1]), lambda i: (i, 0))
     seq = lambda w: pl.BlockSpec((1, seq_len, w), lambda i: (i, 0, 0))
     return pl.pallas_call(
-        back_kernel, grid=(seqs,), out_shape=(sds(qkv.shape), sds(d_x1.shape)),
-        in_specs=[seq(hidden), seq(width), seq(seq_len), any_spec(), pl.BlockSpec(wo.shape, lambda i: (0, 0))],
-        out_specs=(seq(width), seq(hidden)),
+        back_kernel, grid=(seqs,), out_shape=(sds(qkv.shape), sds(d_x1.shape), sds(g_up.shape), sds(g_down.shape)),
+        in_specs=[seq(hidden), seq(width), seq(seq_len), any_spec(), pl.BlockSpec(wo.shape, lambda i: (0, 0)), part(g_up), part(g_down)],
+        out_specs=(seq(width), seq(hidden), part(g_up), part(g_down)),
         scratch_shapes=[pltpu.VMEM((hidden, width), BF16), pltpu.SemaphoreType.DMA((wq.shape[0],))],
         compiler_params=pltpu.CompilerParams(vmem_limit_bytes=VMEM_BYTES),
-        cost_estimate=pl.CostEstimate(flops=20 * 10 ** 9, bytes_accessed=30 * 10 ** 6, transcendentals=0))(d_x1, qkv, keep, wq, wo)
+        cost_estimate=pl.CostEstimate(flops=20 * 10 ** 9, bytes_accessed=30 * 10 ** 6, transcendentals=0))(d_x1, qkv, keep, wq, wo, g_up, g_down)
+
+
+def put_kernel(*refs):
+    half = len(refs) // 2
+    for source, target in zip(refs[:half], refs[half:]):
+        target[...] = source[...]
+
+
+def put_call(*arrays):
+    steps = 8
+
+    def spec(v):
+        axis = max(range(v.ndim - 1), key=lambda k: v.shape[k])
+        shape = tuple(n // steps if k == axis else n for k, n in enumerate(v.shape))
+        return pl.BlockSpec(shape, lambda i: tuple(i if k == axis else 0 for k in range(v.ndim)))
+    specs = [spec(v) for v in arrays]
+    return pl.pallas_call(put_kernel, grid=(steps,), out_shape=tuple(sds(v.shape, v.dtype) for v in arrays), in_specs=specs, out_specs=tuple(specs),
+                          compiler_params=pltpu.CompilerParams(vmem_limit_bytes=VMEM_BYTES),
+                          cost_estimate=pl.CostEstimate(flops=10 ** 6, bytes_accessed=60 * 10 ** 6, transcendentals=0))(*arrays)
 
 
 def dot_of(spec, lhs, rhs):
@@ -628,29 +707,27 @@
         heads, dim = w_qkv.shape[1], w_qkv.shape[3]
         at_pos = lax.broadcasted_iota(jnp.int32, (seq_len, seq_len), 0) >= lax.broadcasted_iota(jnp.int32, (seq_len, seq_len), 1)
         keep = ((seg_ids[:, :, None] == seg_ids[:, None, :]) & at_pos[None]).astype(F32)
-        gain_a = gain_attn.astype(F32)[None]
-        gain_m = gain_mlp.astype(F32)[None]
+        gain_a, gain_m = gain_attn[None], gain_mlp[None]
         wq = jnp.transpose(w_qkv, (1, 2, 0, 3)).reshape(heads * 3, hidden, dim)
         wo = w_out.reshape(heads * dim, hidden)
         flat = lambda v: v.reshape(row_count, v.shape[-1])
 
-        p1 = first_call(tokens, keep, gain_a, wq, wo)
-        b_full, x1_rows, normed, qkv, heads_out, p1_again = ka_call(p1, tokens, keep, gain_a, gain_m, wq, wo, 0)
-        b_again, x1_again, p2 = kb_call(p1_again, tokens, b_full, gain_m, w_up, w_down, 1)
+        b_full, x1_rows, normed, qkv, heads_out, p1_again = ka_call(tokens, keep, gain_a, gain_m, wq, wo, 0)
+        b_again, x1_again, p2, d_hidden = kb_call(p1_again, tokens, b_full, d_out, gain_m, w_up, w_down, 1)
         p2_rows = lax.psum_scatter(flat(p2), AXIS, scatter_dimension=0, tiled=True)
         out_rows = (x1_rows.astype(F32) + p2_rows.astype(F32)).astype(BF16)
 
         pre_act = dot_of('rh,hf->rf', flat(b_again), w_up)
         hidden_act, gelu_back = jax.vjp(gelu, pre_act)
         hidden_act = hidden_act.astype(BF16)
-        d_hidden = dot_of('rh,fh->rf', flat(d_out), w_down).astype(BF16)
-        d_pre = gelu_back(d_hidden.astype(F32))[0].astype(BF16)
+        d_pre = gelu_back(flat(d_hidden).astype(F32))[0].astype(BF16)
         d_b = dot_of('rf,hf->rh', d_pre, w_up).astype(BF16).reshape(tokens.shape)
         d_x1, d_gain_m, d_w_up, d_w_down = grad_call(d_b, x1_again, d_out, gain_m, flat(b_again), d_pre, hidden_act, flat(d_out), 1, 2)
         d_x1, out_rows = lax.optimization_barrier((d_x1, out_rows))
         layer_out = lax.all_gather(out_rows, AXIS, axis=0, tiled=True).reshape(tokens.shape)
-        d_qkv, d_a = back_call(d_x1, qkv, keep, wq, wo)
+        d_qkv, d_a, d_w_up, d_w_down = back_call(d_x1, qkv, keep, wq, wo, d_w_up, d_w_down)
         d_tokens, d_gain, d_wq, d_wo = grad_call(d_a, tokens, d_x1, gain_a, flat(normed), flat(d_qkv), flat(heads_out), flat(d_x1), heads * 3, 3, d_gain_m)
+        layer_out, d_tokens, d_wq, d_wo = put_call(layer_out, d_tokens, d_wq, d_wo)
         d_w_qkv = jnp.transpose(d_wq.reshape(heads, 3, hidden, dim), (2, 0, 1, 3))
         d_w_out = d_wo.reshape(w_out.shape)
         d_gain_a, d_gain_m = d_gain[0, :hidden], d_gain[0, hidden:]

time: 562 us -> 510 us (0.907)
  local copies, waits for them, and re-layouts: 33.5 us -> 3.95 us
  matrix products: 51.5 us -> 32.5 us
    unnamed x24 -> x8, local copies, waits for them, and re-layouts: 32.1 us -> 0.02 us
    pallas_call x1, Pallas kernels: 42.1 us -> 19.6 us  [put_call(): pl.pallas_call(put_kernel, grid=(steps,), out_shape=tuple((sds(v.shape, v...]
    dot_general x3 -> x2, matrix products: 51.5 us -> 32.5 us  [dot_of(): return jnp.einsum(spec, lhs, rhs, preferred_element_type=F32)]
    pallas_call x1, Pallas kernels: 90.3 us -> 106 us  [ka_call(): pl.pallas_call(ka_kernel, out_shape=(full(hidden), sds((seq_len, hidden))...]
    pallas_call x2, Pallas kernels: 182 us -> 189 us  [grad_call(): pl.pallas_call(functools.partial(grad_kernel, last), out_shape=outs, in_s...]
  transfers between devices with their start and end apart: 2 -> 2, of which waited for: 0 -> 0; matrix products, arithmetic and copies ran while one was open for 10% -> 7% of each run, Pallas kernels for 41% -> 46%
where the time goes in v2:
time: 510 us; the launch traced here: 501 us
  Pallas kernels  445 us (87%)
  matrix products  32.5 us (6%)
  between operations  14.6 us (3%)
    pallas_call x2, Pallas kernels, grad_call(): pl.pallas_call(functools.partial(grad_kernel, last), out_shape=outs, in_s...  189 us
    pallas_call x1, Pallas kernels, ka_call(): pl.pallas_call(ka_kernel, out_shape=(full(hidden), sds((seq_len, hidden))...  106 us
    pallas_call x1, Pallas kernels, kb_call(): pl.pallas_call(kb_kernel, out_shape=(sds(tokens.shape), sds((seq_len, hid...  86.9 us
    pallas_call x1, Pallas kernels, back_call(): pl.pallas_call(back_kernel, grid=(seqs,), out_shape=(sds(qkv.shape), sds(...  44.1 us
    dot_general x2, matrix products, dot_of(): return jnp.einsum(spec, lhs, rhs, preferred_element_type=F32)  32.5 us
    pallas_call x1, Pallas kernels, put_call(): pl.pallas_call(put_kernel, grid=(steps,), out_shape=tuple((sds(v.shape, v...  19.6 us
  transfers between devices with their start and end apart: 2, of which 0 were waited for; matrix products, arithmetic and copies ran while one was open for 7% of the time, Pallas kernels for 46%

profile of v2, /device:TPU:113, one launch (start us, length us, event | category | flops | bytes accessed | tf_op | source)
XLA Modules:
  0.0 501.2 jit_solution(18091231576740428381)
XLA Ops:
  7.2 0.1 reduce-scatter.2.cloned.1.call-start
  7.3 1.3 broadcast_in_dim.10.gain_m.gain
  8.6 1.3 broadcast_in_dim.4.gain_a.gain
  9.9 2.2 and_convert_fusion.keep
  12.1 105.7 %shard_map.152 = (bf16[8,192,3072]{2,1,0:T(8,128)(2,1)}, bf16[192,3072]{1,0:T(8,128)(2,1)}, bf16[8,192,3072]{2,1,0:T(8,128)(2,1)}, bf16[8,192,1152]{2,1,0:T(8,12...) custom-call(bf16[8,192,3072]{2,1,0:T(8,128)(2,1)} %values.1, f32[8,192,192]{2,1,0:T(8,128)} %and_convert_fusion.keep, ...), custom_call_target="tpu_custom_call" | custom-call | flops 80000000000 | bytes 80000000 | tf_op jit(solution)/shard_map/pallas_call | solution.py:455
  117.7 86.9 %shard_map.153 = (bf16[8,192,3072]{2,1,0:T(8,128)(2,1)}, bf16[192,3072]{1,0:T(8,128)(2,1)}, bf16[8,192,3072]{2,1,0:T(8,128)(2,1)}, bf16[8,192,1024]{2,1,0:T(8,128)(2,1)}) custom-call(bf16[8,192,3072]{2,1,0:T(8,128)(2,1)} %get-tuple-element.36.p1, bf16[8,192,3072]{2,1,0:T(8,128)(2,1)} %values.1, bf16[8,192,3072]{2,1,0:T(8,128)(2,1)} %get-tuple-element.37.b_fwd, ...), custom_call_target="tpu_custom_call" | custom-call | flops 80000000000 | bytes 80000000 | tf_op jit(solution)/shard_map/pallas_call | solution.py:507
  204.7 0.0 slice-start
  204.7 0.1 reduce-scatter.2.cloned.1.call-update
  204.8 0.1 all-gather.2.cloned.1.call-start
  204.8 0.0 slice-start.1
  204.8 20.3 %multiply_convert_fusion = (bf16[1536,1024]{1,0:T(8,128)(2,1)}, bf16[1536,1024]{1,0:T(8,128)(2,1)S(1)}) fusion(bf16[8,192,1024]{2,1,0:T(8,128)(2,1)} %get-tuple-element.38, bf16[1536,3072]{1,0:T(8,128)(2,1)} %bitcast.41, bf16[3072,1024]{1,0:T(8,128)(2,1)} %up_hbm.1), kind=kOutput, calls=%fused_computation.15 | convolution fusion | flops 9699852288 | bytes 25165824 | tf_op jit(solution)/shard_map/rh,hf->rf/dot_general | solution.py:700
  225.1 0.0 slice-done
  225.1 0.0 slice-done.1
  225.1 12.2 %convolution_convert_fusion = bf16[1536,3072]{1,0:T(8,128)(2,1)} fusion(bf16[1536,1024]{1,0:T(8,128)(2,1)S(1)} %get-tuple-element.65.wide_r, bf16[3072,1024]{1,0:T(8,128)(2,1)S(1)} %bitcast.35), kind=kOutput, calls=%fused_computation | convolution fusion | flops 9668395008 | bytes 18874368 | tf_op jit(solution)/shard_map/rf,hf->rh/dot_general | solution.py:700
  237.4 0.0 copy-done.1
  237.4 100.1 %shard_map.154 = (bf16[8,192,3072]{2,1,0:T(8,128)(2,1)}, f32[1,3072]{1,0:T(1,128)}, bf16[3072,1024]{1,0:T(8,128)(2,1)}, bf16[1024,3072]{1,0:T(8,128)(2,1)}) custom-call(bf16[8,192,3072]{2,1,0:T(8,128)(2,1)} %bitcast.43, bf16[192,3072]{1,0:T(8,128)(2,1)} %get-tuple-element.40.values, bf16[8,192,3072]{2,1,0:T(8,128)(2,1)} %resid.1, ...), custom_call_target="tpu_custom_call" | custom-call | flops 80000000000 | bytes 80000000 | tf_op jit(solution)/shard_map/pallas_call | solution.py:645
  337.5 0.0 reduce-scatter.2.cloned.1.call-done
  337.5 0.0 copy-done
  337.5 2.7 add_convert_fusion
  340.2 0.1 all-gather.2.cloned.1.call-update
  340.3 44.1 %shard_map.155 = (bf16[8,192,1152]{2,1,0:T(8,128)(2,1)}, bf16[8,192,3072]{2,1,0:T(8,128)(2,1)}, bf16[3072,1024]{1,0:T(8,128)(2,1)}, bf16[1024,3072]{1,0:T(8,128)(2,1)}) custom-call(bf16[8,192,3072]{2,1,0:T(8,128)(2,1)} %get-tuple-element.45.d_x1.resid, bf16[8,192,1152]{2,1,0:T(8,128)(2,1)} %get-tuple-element.46.qkv, f32[8,192,192]{2,1,0:T(8,128)} %and_convert_fusion.keep, ...), custom_call_target="tpu_custom_call" | custom-call | flops 20000000000 | bytes 30000000 | tf_op jit(solution)/shard_map/pallas_call | solution.py:671
  384.4 88.6 %shard_map.156 = (bf16[8,192,3072]{2,1,0:T(8,128)(2,1)}, f32[1,6144]{1,0:T(1,128)}, bf16[9,3072,128]{2,1,0:T(8,128)(2,1)}, bf16[384,3072]{1,0:T(8,128)(2,1)}) custom-call(bf16[8,192,3072]{2,1,0:T(8,128)(2,1)} %get-tuple-element.49.part, bf16[8,192,3072]{2,1,0:T(8,128)(2,1)} %values.1, bf16[8,192,3072]{2,1,0:T(8,128)(2,1)} %get-tuple-element.45.d_x1.resid, ...), custom_call_target="tpu_custom_call" | custom-call | flops 80000000000 | bytes 80000000 | tf_op jit(solution)/shard_map/pallas_call | solution.py:645
  473.0 1.3 fusion.10
  474.3 19.6 %shard_map.157 = (bf16[8,192,3072]{2,1,0:T(8,128)(2,1)}, bf16[8,192,3072]{2,1,0:T(8,128)(2,1)}, bf16[9,3072,128]{2,1,0:T(8,128)(2,1)}, bf16[384,3072]{1,0:T(8,128)(2,1)}) custom-call(bf16[8,192,3072]{2,1,0:T(8,128)(2,1)} %bitcast.26, bf16[8,192,3072]{2,1,0:T(8,128)(2,1)} %get-tuple-element.54.refs_1_, bf16[9,3072,128]{2,1,0:T(8,128)(2,1)} %get-tuple-element.55.refs_2_, ...), custom_call_target="tpu_custom_call" | custom-call | flops 1000000 | bytes 60000000 | tf_op jit(solution)/shard_map/pallas_call | solution.py:694
  (5 shorter events, 0.0 us)
Async XLA Ops:
  7.2 330.3 %reduce-scatter.2.cloned.1.call-start = ((), (), s32[]{:S(2)}) async-start(), calls=%async_computation.1 | async-start | bytes 10616832 | tf_op jit(solution)/shard_map/reduce_scatter | solution.py:717
  204.7 20.4 %slice-start = ((s8[6291456]{0:T(1024)(128)(4,1)}), s8[2097152]{0:T(1024)(128)(4,1)S(1)}, s32[]{:S(2)}) async-start(s8[6291456]{0:T(1024)(128)(4,1)} %bitcast.34), calls=%async_computation.3 | async-start | bytes 4194304
  204.8 269.5 %all-gather.2.cloned.1.call-start = ((), (), s32[]{:S(2)}) async-start(), calls=%async_computation.2 | async-start | bytes 10616832 | tf_op jit(solution)/shard_map/all_gather | solution.py:727
  204.8 20.3 %slice-start.1 = ((s8[6291456]{0:T(1024)(128)(4,1)}), s8[4194304]{0:T(1024)(128)(4,1)S(1)}, s32[]{:S(2)}) async-start(s8[6291456]{0:T(1024)(128)(4,1)} %bitcast.34), calls=%async_computation.4 | async-start | bytes 8388608
  225.1 12.2 %copy-start.1 = (bf16[1536,1024]{1,0:T(8,128)(2,1)}, bf16[1536,1024]{1,0:T(8,128)(2,1)S(1)}, u32[]{:S(2)}) copy-start(bf16[1536,1024]{1,0:T(8,128)(2,1)S(1)} %get-tuple-element.65.wide_r) | copy-start | bytes 9437188
  237.4 100.1 %copy-start = (bf16[192,3072]{1,0:T(8,128)(2,1)S(1)}, bf16[192,3072]{1,0:T(8,128)(2,1)}, u32[]{:S(2)}) copy-start(bf16[192,3072]{1,0:T(8,128)(2,1)} %get-tuple-element.42) | copy-start | bytes 3538948
Sparse Core Ops, SparseCore 0:
  204.9 82.8 reduce-scatter.1
  340.4 50.4 all-gather.1
